TPU v7x, 256 devices: a whole 4x4x8 slice. The times are simulated.
256 devices in a mesh: mkt: 8 (over z), prod: 2 (over core), draw: 16 (over y, x).
Axes of the slice: x: 4, y: 4, z: 8, core: 2. Of those that a mesh axis runs over, the one named last changes fastest.
Arguments:
- start_utility: float32 [2048, 256], P('mkt', 'prod'), may hold values from -5 to -2
- log_shares: float32 [2048, 256], P('mkt', 'prod'), may hold values from -9 to -5
- characteristics: float32 [2048, 8, 256], P('mkt', None, 'prod'), may hold values from -2.5 to 2.5
- coef_scale: float32 [8], replicated, may hold values from 0.1 to 0.3
- taste_draws: float32 [2048, 8, 2048], P('mkt', None, 'draw'), may hold values from -2.5 to 2.5
Outputs:
- mean_utility: float32 [2048, 256], P('mkt', 'prod')
- step_norms: float32 [2], replicated
All inputs are finite; a program needn't handle non-finite values.
Results may differ from a plain program's by a relative error of at most 0.0001.
Values sent between devices are 32-bit elements; how exact they have to be, the bound alone decides.
No kernel may reach another device: no remote copies, remote signals or barrier semaphores. Data moves between devices by JAX's collectives and lax.ppermute only.
A program may use at most 64 MiB of HBM per device.

v0:
```python
import math

import jax
import jax.numpy as jnp
from jax import lax
from jax.sharding import PartitionSpec as P

R = 2048
ITERS = 2


def gathered_total(shard, axis):
    return lax.all_gather(shard, axis).sum(0)


def split_up(shard, dim, count):
    shape = shard.shape
    tiles = shard.reshape(*shape[:dim], count, shape[dim] // count, *shape[dim + 1 :])
    return jnp.moveaxis(tiles, dim, 0)


def summed_on_arrival(shard, axis, dim):
    count = lax.axis_size(axis)
    tiles = lax.all_to_all(split_up(shard, dim, count), axis, 0, 0, tiled=True)
    return jnp.sum(tiles, axis=0)


def filled_up(lines, count):
    spare = -lines.shape[0] % count
    if not spare:
        return lines
    return jnp.concatenate([lines, jnp.zeros((spare, *lines.shape[1:]), lines.dtype)])


def joined_along(tiles, dim):
    tiles = jnp.moveaxis(tiles, 0, dim)
    shape = tiles.shape
    return tiles.reshape(*shape[:dim], shape[dim] * shape[dim + 1], *shape[dim + 2 :])


def from_everyone(shard, axis):
    copies = jnp.broadcast_to(shard, (lax.axis_size(axis), *shard.shape))
    return lax.all_to_all(copies, axis, split_axis=0, concat_axis=0, tiled=True)


def gather_directly(shard, axis, dim):
    return joined_along(from_everyone(shard, axis), dim)


def total_of(shard, axes):
    lines = shard.reshape(-1, shard.shape[-1])
    own = summed_on_arrival(filled_up(lines, lax.axis_size(axes)), axes, 0)
    whole = gather_directly(own, axes, 0)
    return whole[: len(lines)].reshape(shard.shape)


def taken_together(shard, axis):
    everything = from_everyone(shard, axis)
    return jnp.sum(everything, axis=0)


def exponent(chars_part, scaled_part, util_part):
    spread = jnp.einsum("mkj,mkr->mjr", chars_part, scaled_part, precision=lax.Precision.HIGHEST)
    return jnp.exp(util_part[:, :, None] + spread)


def shards(start_utility, log_shares, characteristics, coef_scale, taste_draws):
    markets, coef_count, local_prod = characteristics.shape
    local_draws = taste_draws.shape[2]
    scaled = taste_draws * coef_scale[None, :, None]
    block_size = math.gcd(markets, 64)
    block_count = markets // block_size
    scaled_blocks = scaled.reshape(block_count, block_size, coef_count, local_draws)
    char_blocks = characteristics.reshape(block_count, block_size, coef_count, local_prod)
    utility = start_utility
    partials = []
    for iteration in range(ITERS):
        util_blocks = utility.reshape(block_count, block_size, local_prod)

        def sum_exp(inputs):
            chars_part, scaled_part, util_part = inputs
            return jnp.sum(exponent(chars_part, scaled_part, util_part), axis=1)

        local_sums = lax.map(sum_exp, (char_blocks, scaled_blocks, util_blocks))
        totals_exp = gathered_total(local_sums.reshape(markets, local_draws), "prod")

        def share_pass(inputs):
            chars_part, scaled_part, util_part, total_part = inputs
            exp_util = exponent(chars_part, scaled_part, util_part)
            return jnp.sum(exp_util / (1.0 + total_part[:, None, :]), axis=2)

        summed = lax.map(
            share_pass,
            (
                char_blocks,
                scaled_blocks,
                util_blocks,
                totals_exp.reshape(block_count, block_size, local_draws),
            ),
        )
        predicted = total_of(summed.reshape(markets, local_prod), "draw") / R
        updated = utility + log_shares - jnp.log(predicted)
        change = updated - utility
        square_sum = jnp.sum(change * change)
        partials.append(square_sum)
        utility = updated
    totals = taken_together(jnp.stack(partials), ("mkt", "prod"))
    cell_count = markets * local_prod * lax.axis_size("mkt") * lax.axis_size("prod")
    step_norms = jnp.sqrt(totals / cell_count + 1e-06)
    return (utility, step_norms)


def solution(mesh):
    return jax.shard_map(
        shards,
        mesh=mesh,
        in_specs=(
            P("mkt", "prod"),
            P("mkt", "prod"),
            P("mkt", None, "prod"),
            P(),
            P("mkt", None, "draw"),
        ),
        out_specs=(P("mkt", "prod"), P()),
        check_vma=False,
    )
```

profile of v0, /device:TPU:1, one launch (start us, length us, event | category | flops | bytes accessed | tf_op | source)
XLA Modules:
  0.0 202.7 jit_solution(9859128783336821165)
XLA Ops:
  0.6 0.0 copy-start
  0.6 0.0 copy-start.2
  0.7 1.5 broadcast_multiply_fusion
  2.1 0.0 copy-done
  2.1 0.1 copy-done.2
  2.3 31.6 %while.40 = (s32[]{:T(128)}, f32[4,64,128]{2,1,0:T(8,128)S(1)}, f32[4,64,128]{2,1,0:T(8,128)S(1)}, f32[4,64,8,128]{3,2,1,0:T(8,128)S(1)}, f32[4,64,8,128]{3,2,1,0:T(8,128)S(1)}, /*index=5*/s32[]{:T(128)}) while((s32[]{:T(128)}, f32[4,64,128]{2,1,0:T(8,128)S(1)}, f32[4,64,128]{2,1,0:T(8,128)S(1)}, f32[4,64,8,128]{3,2,1,0:T(8,128)S(1)}, ...), condition=%wide.region_2.3_spmd, body=%wide.region_0.2_spmd.sunk | while | flops 102752256 | bytes 721997 | solution.py:84
  2.3 7.8 %exponential_reduce_fusion.4 = f32[64,128]{1,0:T(8,128)S(1)} fusion(f32[64,128]{1,0:T(8,128)S(1)} %dynamic-slice_bitcast_fusion.6, f32[4,64,8,128]{3,2,1,0:T(8,128)S(1)} %get-tuple-element.335, s32[]{:T(128)} %get-tuple-element.325, f32[4,64,8,128]{3,2,1,0:T(8,128)S(1)} %get-tuple-element.334), kind=kOutput, calls=%fused_computation.clone.1 | convolution fusion | flops 102752256 | bytes 590848 | tf_op jit(solution)/shard_map/while/body/eval_jaxpr/mkj,mkr->mjr/dot_general | solution.py:63
  10.2 7.8 %exponential_reduce_fusion.4 = f32[64,128]{1,0:T(8,128)S(1)} fusion(f32[64,128]{1,0:T(8,128)S(1)} %dynamic-slice_bitcast_fusion.6, f32[4,64,8,128]{3,2,1,0:T(8,128)S(1)} %get-tuple-element.335, s32[]{:T(128)} %get-tuple-element.325, f32[4,64,8,128]{3,2,1,0:T(8,128)S(1)} %get-tuple-element.334), kind=kOutput, calls=%fused_computation.clone.1 | convolution fusion | flops 102752256 | bytes 590848 | tf_op jit(solution)/shard_map/while/body/eval_jaxpr/mkj,mkr->mjr/dot_general | solution.py:63
  18.1 7.8 %exponential_reduce_fusion.4 = f32[64,128]{1,0:T(8,128)S(1)} fusion(f32[64,128]{1,0:T(8,128)S(1)} %dynamic-slice_bitcast_fusion.6, f32[4,64,8,128]{3,2,1,0:T(8,128)S(1)} %get-tuple-element.335, s32[]{:T(128)} %get-tuple-element.325, f32[4,64,8,128]{3,2,1,0:T(8,128)S(1)} %get-tuple-element.334), kind=kOutput, calls=%fused_computation.clone.1 | convolution fusion | flops 102752256 | bytes 590848 | tf_op jit(solution)/shard_map/while/body/eval_jaxpr/mkj,mkr->mjr/dot_general | solution.py:63
  26.0 7.8 %exponential_reduce_fusion.4 = f32[64,128]{1,0:T(8,128)S(1)} fusion(f32[64,128]{1,0:T(8,128)S(1)} %dynamic-slice_bitcast_fusion.6, f32[4,64,8,128]{3,2,1,0:T(8,128)S(1)} %get-tuple-element.335, s32[]{:T(128)} %get-tuple-element.325, f32[4,64,8,128]{3,2,1,0:T(8,128)S(1)} %get-tuple-element.334), kind=kOutput, calls=%fused_computation.clone.1 | convolution fusion | flops 102752256 | bytes 590848 | tf_op jit(solution)/shard_map/while/body/eval_jaxpr/mkj,mkr->mjr/dot_general | solution.py:63
  33.8 4.8 %all_gather.6 = f32[2,256,128]{2,1,0:T(8,128)S(1)} all-gather(f32[1,256,128]{2,1,0:T(8,128)S(1)} %bitcast.101), channel_id=1, replica_groups=mesh['mkt'=8,'prod'=2,'draw'=16] {'prod'}, dimensions={0}, use_global_device_ids=true | all-gather | bytes 393216 | tf_op jit(solution)/shard_map/all_gather | solution.py:13
  38.7 31.6 %while.41 = (s32[]{:T(128)}, f32[4,64,128]{2,1,0:T(8,128)S(1)}, f32[4,64,128]{2,1,0:T(8,128)S(1)}, f32[4,64,8,128]{3,2,1,0:T(8,128)S(1)}, f32[4,64,8,128]{3,2,1,...) while((s32[]{:T(128)}, f32[4,64,128]{2,1,0:T(8,128)S(1)}, f32[4,64,128]{2,1,0:T(8,128)S(1)}, ...), condition=%wide.region_6.7_spmd, body=%wide.region_4.6_spmd.sunk | while | flops 103809024 | bytes 820309 | solution.py:92
  38.7 7.9 %fusion.36 = f32[64,128]{1,0:T(8,128)S(1)} fusion(f32[64,128]{1,0:T(8,128)S(1)} %get-tuple-element.304, f32[64,128]{1,0:T(8,128)S(1)} %get-tuple-element.305, f32[4,64,8,128]{3,2,1,0:T(8,128)S(1)} %get-tuple-element.355, s32[]{:T(128)} %get-tuple-element.344, f32[4,64,8,128]{3,2,1,0:T(8,128)S(1)} %get-tuple-element.354), kind=kOutput, calls=%fused_computation.9.clone.1 | convolution fusion | flops 103800832 | bytes 623616 | tf_op jit(solution)/shard_map/while/body/eval_jaxpr/mkj,mkr->mjr/dot_general | solution.py:63
  46.7 7.9 %fusion.36 = f32[64,128]{1,0:T(8,128)S(1)} fusion(f32[64,128]{1,0:T(8,128)S(1)} %get-tuple-element.304, f32[64,128]{1,0:T(8,128)S(1)} %get-tuple-element.305, f32[4,64,8,128]{3,2,1,0:T(8,128)S(1)} %get-tuple-element.355, s32[]{:T(128)} %get-tuple-element.344, f32[4,64,8,128]{3,2,1,0:T(8,128)S(1)} %get-tuple-element.354), kind=kOutput, calls=%fused_computation.9.clone.1 | convolution fusion | flops 103800832 | bytes 623616 | tf_op jit(solution)/shard_map/while/body/eval_jaxpr/mkj,mkr->mjr/dot_general | solution.py:63
  54.6 7.9 %fusion.36 = f32[64,128]{1,0:T(8,128)S(1)} fusion(f32[64,128]{1,0:T(8,128)S(1)} %get-tuple-element.304, f32[64,128]{1,0:T(8,128)S(1)} %get-tuple-element.305, f32[4,64,8,128]{3,2,1,0:T(8,128)S(1)} %get-tuple-element.355, s32[]{:T(128)} %get-tuple-element.344, f32[4,64,8,128]{3,2,1,0:T(8,128)S(1)} %get-tuple-element.354), kind=kOutput, calls=%fused_computation.9.clone.1 | convolution fusion | flops 103800832 | bytes 623616 | tf_op jit(solution)/shard_map/while/body/eval_jaxpr/mkj,mkr->mjr/dot_general | solution.py:63
  62.5 7.9 %fusion.36 = f32[64,128]{1,0:T(8,128)S(1)} fusion(f32[64,128]{1,0:T(8,128)S(1)} %get-tuple-element.304, f32[64,128]{1,0:T(8,128)S(1)} %get-tuple-element.305, f32[4,64,8,128]{3,2,1,0:T(8,128)S(1)} %get-tuple-element.355, s32[]{:T(128)} %get-tuple-element.344, f32[4,64,8,128]{3,2,1,0:T(8,128)S(1)} %get-tuple-element.354), kind=kOutput, calls=%fused_computation.9.clone.1 | convolution fusion | flops 103800832 | bytes 623616 | tf_op jit(solution)/shard_map/while/body/eval_jaxpr/mkj,mkr->mjr/dot_general | solution.py:63
  70.4 0.0 copy-start.1
  70.4 11.8 %all_to_all.27 = f32[16,16,128]{2,1,0:T(8,128)S(1)} all-to-all(f32[16,16,128]{2,1,0:T(8,128)S(1)} %bitcast.103), channel_id=1, replica_groups=mesh['mkt'=8,'prod'=2,'draw'=16] {'draw'}, dimensions={0} | all-to-all | bytes 262144 | tf_op jit(solution)/shard_map/all_to_all | solution.py:24
  82.2 0.7 broadcast_in_dim.29
  82.9 3.5 %all-to-all-start.1 = ((f32[16,16,128]{2,1,0:T(8,128)}), f32[16,16,128]{2,1,0:T(8,128)S(1)}, u32[]{:S(2)}, u32[]{:S(2)}) async-start(f32[16,16,128]{2,1,0:T(8,128)} %broadcast_in_dim.29), calls=%async_computation.1 | async-start | bytes 262144 | tf_op jit(solution)/shard_map/all_to_all | solution.py:43
  86.4 6.8 %all-to-all-done.1 = f32[16,16,128]{2,1,0:T(8,128)S(1)} async-done(((f32[16,16,128]{2,1,0:T(8,128)}), f32[16,16,128]{2,1,0:T(8,128)S(1)}, u32[]{:S(2)}, u32[]{:S(2)}) %all-to-all-start.1) | async-done | bytes 131104 | tf_op jit(solution)/shard_map/all_to_all | solution.py:43
  93.2 0.0 copy-done.1
  93.3 31.6 %while.42 = (s32[]{:T(128)}, f32[4,64,128]{2,1,0:T(8,128)S(1)}, f32[4,64,128]{2,1,0:T(8,128)S(1)}, f32[4,64,8,128]{3,2,1,0:T(8,128)S(1)}, f32[4,64,8,128]{3,2,1,0:T(8,128)S(1)}, /*index=5*/s32[]{:T(128)}) while((s32[]{:T(128)}, f32[4,64,128]{2,1,0:T(8,128)S(1)}, f32[4,64,128]{2,1,0:T(8,128)S(1)}, f32[4,64,8,128]{3,2,1,0:T(8,128)S(1)}, ...), condition=%wide.region_10.11_spmd, body=%wide.region_8.10_spmd.sunk | while | flops 102752256 | bytes 721997 | solution.py:84
  93.3 7.9 %exponential_reduce_fusion.5 = f32[64,128]{1,0:T(8,128)S(1)} fusion(f32[64,128]{1,0:T(8,128)S(1)} %dynamic-slice_bitcast_fusion.7, f32[4,64,8,128]{3,2,1,0:T(8,128)S(1)} %get-tuple-element.374, s32[]{:T(128)} %get-tuple-element.364, f32[4,64,8,128]{3,2,1,0:T(8,128)S(1)} %get-tuple-element.373), kind=kOutput, calls=%fused_computation.18.clone.1 | convolution fusion | flops 102752256 | bytes 590848 | tf_op jit(solution)/shard_map/while/body/eval_jaxpr/mkj,mkr->mjr/dot_general | solution.py:63
  101.2 7.9 %exponential_reduce_fusion.5 = f32[64,128]{1,0:T(8,128)S(1)} fusion(f32[64,128]{1,0:T(8,128)S(1)} %dynamic-slice_bitcast_fusion.7, f32[4,64,8,128]{3,2,1,0:T(8,128)S(1)} %get-tuple-element.374, s32[]{:T(128)} %get-tuple-element.364, f32[4,64,8,128]{3,2,1,0:T(8,128)S(1)} %get-tuple-element.373), kind=kOutput, calls=%fused_computation.18.clone.1 | convolution fusion | flops 102752256 | bytes 590848 | tf_op jit(solution)/shard_map/while/body/eval_jaxpr/mkj,mkr->mjr/dot_general | solution.py:63
  109.1 7.9 %exponential_reduce_fusion.5 = f32[64,128]{1,0:T(8,128)S(1)} fusion(f32[64,128]{1,0:T(8,128)S(1)} %dynamic-slice_bitcast_fusion.7, f32[4,64,8,128]{3,2,1,0:T(8,128)S(1)} %get-tuple-element.374, s32[]{:T(128)} %get-tuple-element.364, f32[4,64,8,128]{3,2,1,0:T(8,128)S(1)} %get-tuple-element.373), kind=kOutput, calls=%fused_computation.18.clone.1 | convolution fusion | flops 102752256 | bytes 590848 | tf_op jit(solution)/shard_map/while/body/eval_jaxpr/mkj,mkr->mjr/dot_general | solution.py:63
  117.0 7.9 %exponential_reduce_fusion.5 = f32[64,128]{1,0:T(8,128)S(1)} fusion(f32[64,128]{1,0:T(8,128)S(1)} %dynamic-slice_bitcast_fusion.7, f32[4,64,8,128]{3,2,1,0:T(8,128)S(1)} %get-tuple-element.374, s32[]{:T(128)} %get-tuple-element.364, f32[4,64,8,128]{3,2,1,0:T(8,128)S(1)} %get-tuple-element.373), kind=kOutput, calls=%fused_computation.18.clone.1 | convolution fusion | flops 102752256 | bytes 590848 | tf_op jit(solution)/shard_map/while/body/eval_jaxpr/mkj,mkr->mjr/dot_general | solution.py:63
  124.9 4.8 %all_gather.7 = f32[2,256,128]{2,1,0:T(8,128)S(1)} all-gather(f32[1,256,128]{2,1,0:T(8,128)S(1)} %bitcast.102), channel_id=1, replica_groups=mesh['mkt'=8,'prod'=2,'draw'=16] {'prod'}, dimensions={0}, use_global_device_ids=true | all-gather | bytes 393216 | tf_op jit(solution)/shard_map/all_gather | solution.py:13
  129.7 31.7 %while.43 = (s32[]{:T(128)}, f32[4,64,128]{2,1,0:T(8,128)S(1)}, f32[4,64,128]{2,1,0:T(8,128)S(1)}, f32[4,64,8,128]{3,2,1,0:T(8,128)S(1)}, f32[4,64,8,128]{3,2,1,...) while((s32[]{:T(128)}, f32[4,64,128]{2,1,0:T(8,128)S(1)}, f32[4,64,128]{2,1,0:T(8,128)S(1)}, ...), condition=%wide.region_14.15_spmd, body=%wide.region_12.14_spmd.sunk | while | flops 103809024 | bytes 820309 | solution.py:92
  129.8 7.9 %fusion.41 = f32[64,128]{1,0:T(8,128)S(1)} fusion(f32[64,128]{1,0:T(8,128)S(1)} %get-tuple-element.317, f32[64,128]{1,0:T(8,128)S(1)} %get-tuple-element.318, f32[4,64,8,128]{3,2,1,0:T(8,128)S(1)} %get-tuple-element.394, s32[]{:T(128)} %get-tuple-element.383, f32[4,64,8,128]{3,2,1,0:T(8,128)S(1)} %get-tuple-element.393), kind=kOutput, calls=%fused_computation.27.clone.1 | convolution fusion | flops 103800832 | bytes 623616 | tf_op jit(solution)/shard_map/while/body/eval_jaxpr/mkj,mkr->mjr/dot_general | solution.py:63
  137.7 7.9 %fusion.41 = f32[64,128]{1,0:T(8,128)S(1)} fusion(f32[64,128]{1,0:T(8,128)S(1)} %get-tuple-element.317, f32[64,128]{1,0:T(8,128)S(1)} %get-tuple-element.318, f32[4,64,8,128]{3,2,1,0:T(8,128)S(1)} %get-tuple-element.394, s32[]{:T(128)} %get-tuple-element.383, f32[4,64,8,128]{3,2,1,0:T(8,128)S(1)} %get-tuple-element.393), kind=kOutput, calls=%fused_computation.27.clone.1 | convolution fusion | flops 103800832 | bytes 623616 | tf_op jit(solution)/shard_map/while/body/eval_jaxpr/mkj,mkr->mjr/dot_general | solution.py:63
  145.6 7.9 %fusion.41 = f32[64,128]{1,0:T(8,128)S(1)} fusion(f32[64,128]{1,0:T(8,128)S(1)} %get-tuple-element.317, f32[64,128]{1,0:T(8,128)S(1)} %get-tuple-element.318, f32[4,64,8,128]{3,2,1,0:T(8,128)S(1)} %get-tuple-element.394, s32[]{:T(128)} %get-tuple-element.383, f32[4,64,8,128]{3,2,1,0:T(8,128)S(1)} %get-tuple-element.393), kind=kOutput, calls=%fused_computation.27.clone.1 | convolution fusion | flops 103800832 | bytes 623616 | tf_op jit(solution)/shard_map/while/body/eval_jaxpr/mkj,mkr->mjr/dot_general | solution.py:63
  153.5 7.9 %fusion.41 = f32[64,128]{1,0:T(8,128)S(1)} fusion(f32[64,128]{1,0:T(8,128)S(1)} %get-tuple-element.317, f32[64,128]{1,0:T(8,128)S(1)} %get-tuple-element.318, f32[4,64,8,128]{3,2,1,0:T(8,128)S(1)} %get-tuple-element.394, s32[]{:T(128)} %get-tuple-element.383, f32[4,64,8,128]{3,2,1,0:T(8,128)S(1)} %get-tuple-element.393), kind=kOutput, calls=%fused_computation.27.clone.1 | convolution fusion | flops 103800832 | bytes 623616 | tf_op jit(solution)/shard_map/while/body/eval_jaxpr/mkj,mkr->mjr/dot_general | solution.py:63
  161.5 9.6 %all_to_all.28 = f32[16,16,128]{2,1,0:T(8,128)S(1)} all-to-all(f32[16,16,128]{2,1,0:T(8,128)S(1)} %bitcast.104), channel_id=1, replica_groups=mesh['mkt'=8,'prod'=2,'draw'=16] {'draw'}, dimensions={0} | all-to-all | bytes 262144 | tf_op jit(solution)/shard_map/all_to_all | solution.py:24
  171.1 9.9 %all_to_all.26 = f32[16,16,128]{2,1,0:T(8,128)S(1)} all-to-all(f32[16,16,128]{2,1,0:T(8,128)S(1)} %broadcast_in_dim.30), channel_id=1, replica_groups=mesh['mkt'=8,'prod'=2,'draw'=16] {'draw'}, dimensions={0} | all-to-all | bytes 262144 | tf_op jit(solution)/shard_map/all_to_all | solution.py:43
  181.1 1.4 multiply_reduce_fusion.1
  182.5 1.4 pad_maximum_fusion
  183.9 18.2 %all_to_all.29 = f32[16,1,2]{2,1,0:T(1,128)S(1)} all-to-all(f32[16,1,2]{2,1,0:T(1,128)S(1)} %broadcast_in_dim.31), channel_id=1, replica_groups=mesh['mkt'=8,'prod'=2,'draw'=16] {'mkt','prod'}, dimensions={0} | all-to-all | bytes 256 | tf_op jit(solution)/shard_map/all_to_all | solution.py:43
  202.2 0.5 add_sqrt_fusion
  (46 shorter events, 0.6 us)
Async XLA Ops:
  0.6 1.5 copy-start
  0.6 1.6 copy-start.2
  70.4 22.9 %copy-start.1 = (f32[256,128]{1,0:T(8,128)S(1)}, f32[256,128]{1,0:T(8,128)}, u32[]{:S(2)}) copy-start(f32[256,128]{1,0:T(8,128)} %param.14) | copy-start | bytes 393220
  82.9 10.3 %all-to-all-start.1 = ((f32[16,16,128]{2,1,0:T(8,128)}), f32[16,16,128]{2,1,0:T(8,128)S(1)}, u32[]{:S(2)}, u32[]{:S(2)}) async-start(f32[16,16,128]{2,1,0:T(8,128)} %broadcast_in_dim.29), calls=%async_computation.1 | async-start | bytes 262144 | tf_op jit(solution)/shard_map/all_to_all | solution.py:43
where the time goes:
time: 203 us
  matrix products  126 us (62%)
  blocking collectives  59.2 us (29%)
  waiting for transfers between devices  6.8 us (3%)
  other arithmetic  5.05 us (2%)
  starting transfers between devices  3.51 us (2%)
    dot_general x16, matrix products, exponent(): jnp.einsum('mkj,mkr->mjr', chars_part, scaled_part, precision=lax.Precisi...  126 us
    all_to_all x2, blocking collectives, from_everyone(): return lax.all_to_all(copies, axis, split_axis=0, concat_axis=0, tiled=True)  28.2 us
    all_to_all x2, blocking collectives, summed_on_arrival(): tiles = lax.all_to_all(split_up(shard, dim, count), axis, 0, 0, tiled=True)  21.5 us
    all_gather x2, blocking collectives, gathered_total(): return lax.all_gather(shard, axis).sum(0)  9.58 us
    all_to_all x1, waiting for transfers between devices, from_everyone(): return lax.all_to_all(copies, axis, split_axis=0, concat_axis=0, tiled=True)  6.8 us
  transfers between devices with their start and end apart: 1, of which 1 were waited for; matrix products, arithmetic and copies ran while one was open for 0% of the time, Pallas kernels for 0%

commit v1 on v0

v1 whole, which is shorter than its diff:
```python
import math

import jax
import jax.numpy as jnp
from jax import lax
from jax.experimental import pallas as pl
from jax.experimental.pallas import tpu as pltpu
from jax.sharding import PartitionSpec as P

R = 2048
LOG2E = math.log2(math.e)
LANES = 128
SUBLANES = 8


def rounded(x):
    return x.astype(jnp.bfloat16).astype(jnp.float32)


def first_rows(rows, length):
    width = rows[0].shape[-1]
    index = lax.broadcasted_iota(jnp.int32, (length, width), 0)
    out = jnp.zeros((length, width), jnp.float32)
    for position, row in enumerate(rows):
        out = jnp.where(index == position, jnp.broadcast_to(row, (length, width)), out)
    return out


def three_parts(x):
    high = rounded(x)
    middle = rounded(x - high)
    return high, middle, x - high - middle


def by_first(a, b):
    return lax.dot_general(a, b, (((0,), (0,)), ((), ())), preferred_element_type=jnp.float32)


def by_last(a, b):
    return lax.dot_general(a, b, (((1,), (1,)), ((), ())), preferred_element_type=jnp.float32)


def contraction_kernel(core_ref, coef_ref, own_ref, other_ref, taste_ref, out_ref, weight_ref, inverse_ref, share_ref, factor_ref):
    markets = own_ref.shape[0] // 10
    coefs = 8
    chips = taste_ref.shape[0]
    groups = 2 * LANES // SUBLANES
    core = core_ref[0]

    def part(first, count):
        return jnp.concatenate([own_ref[pl.ds(first, count)], other_ref[pl.ds(first, count)]], axis=1)

    utility = part(8 * markets, markets)
    shares = part(9 * markets, markets)

    coef = jnp.concatenate([jnp.full((1, 2 * LANES), coef_ref[k] * LOG2E, jnp.float32) for k in range(coefs)], axis=0)
    ones = first_rows([jnp.ones((1, 2 * LANES), jnp.float32)] * 3, SUBLANES)

    def all_sublanes(x):
        for shift in (4, 2, 1):
            x = x + pltpu.roll(x, shift, 0)
        return x

    for m in range(markets):
        chars = part(m * coefs, coefs) * coef
        high = rounded(chars)
        base = first_rows(three_parts(utility[m : m + 1] * LOG2E), SUBLANES)
        left = jnp.concatenate([high, high, chars - high, base], axis=0).astype(jnp.bfloat16)
        for t in range(0, chips, 2):
            taste = jnp.concatenate([taste_ref[t, m], taste_ref[t + 1, m]], axis=1)
            taste_high = rounded(taste)
            right = jnp.concatenate([taste_high, taste - taste_high, taste_high, ones], axis=0).astype(jnp.bfloat16)
            weight = jnp.exp2(by_first(left, right))
            for half in range(2):
                piece = weight[:, half * LANES : (half + 1) * LANES]
                weight_ref[m, t + half] = piece
                total = jnp.sum(piece.reshape(groups, SUBLANES, LANES), axis=0)
                inverse_ref[m, t + half] = 1.0 / (1.0 + all_sublanes(total))

    def share_pass():
        predicted = jnp.zeros((SUBLANES, 2 * LANES), jnp.float32)
        row = lax.broadcasted_iota(jnp.int32, (SUBLANES, LANES), 0)

        def one(m, carry):
            inverse = [inverse_ref[m, t] for t in range(chips)]
            for g in range(groups):
                rows = pl.ds(g * SUBLANES, SUBLANES)
                terms = [weight_ref[m, t, rows] * inverse[t] for t in range(chips)]
                while len(terms) > 1:
                    terms = [a + b for a, b in zip(terms[::2], terms[1::2])]
                share_ref[m, rows] = terms[0]
            return carry

        lax.fori_loop(0, markets, one, 0)
        for m in range(markets):
            pick = jnp.where(row == m, 1.0, 0.0).astype(jnp.bfloat16)
            for piece in three_parts(share_ref[m]):
                predicted = predicted + by_last(pick, piece.astype(jnp.bfloat16))
        return predicted

    first_change = shares - jnp.log(share_pass() * (1.0 / R))
    factor = jnp.exp(first_change)
    for m in range(markets):
        left = first_rows(three_parts(factor[m : m + 1]), 2 * SUBLANES).astype(jnp.bfloat16)
        factor_ref[m] = by_first(left, jnp.ones((2 * SUBLANES, LANES), jnp.bfloat16))

    def total_pass(m, carry):
        totals = [jnp.zeros((SUBLANES, LANES), jnp.float32)] * chips
        for g in range(groups):
            rows = pl.ds(g * SUBLANES, SUBLANES)
            scale = factor_ref[m, rows]
            totals = [total + weight_ref[m, t, rows] * scale for t, total in enumerate(totals)]
        for t in range(chips):
            inverse_ref[m, t] = 1.0 / (1.0 + all_sublanes(totals[t]))
        return carry

    lax.fori_loop(0, markets, total_pass, 0)

    second_change = shares - jnp.log(factor * share_pass() * (1.0 / R))
    result = utility + first_change + second_change

    squares = []
    for change in (first_change, second_change):
        square = change * change
        square = square[:, :LANES] + square[:, LANES:]
        squares.append(jnp.sum(square, axis=0, keepdims=True))
    squares = first_rows(squares, SUBLANES)
    for half, place in enumerate((core, 1 - core)):
        block = jnp.concatenate([result[:, half * LANES : (half + 1) * LANES], squares], axis=0)
        out_ref[pl.ds(place * chips, chips)] = jnp.broadcast_to(block, (chips, 2 * SUBLANES, LANES))


def contraction(core, coef_scale, own, other, taste):
    chips, markets, coefs, lanes = taste.shape
    smem = pl.BlockSpec(memory_space=pltpu.SMEM)
    vmem = pl.BlockSpec(memory_space=pltpu.VMEM)
    return pl.pallas_call(
        contraction_kernel,
        out_shape=jax.ShapeDtypeStruct((2 * chips, 2 * SUBLANES, LANES), jnp.float32),
        in_specs=[smem, smem, vmem, vmem, vmem],
        out_specs=vmem,
        scratch_shapes=[
            pltpu.VMEM((markets, chips, 2 * LANES, LANES), jnp.float32),
            pltpu.VMEM((markets, chips, SUBLANES, LANES), jnp.float32),
            pltpu.VMEM((markets, 2 * LANES, LANES), jnp.float32),
            pltpu.VMEM((markets, 2 * LANES, LANES), jnp.float32),
        ],
        compiler_params=pltpu.CompilerParams(vmem_limit_bytes=48 * 1024 * 1024),
    )(core, coef_scale, own, other, taste)


def shards(start_utility, log_shares, characteristics, coef_scale, taste_draws):
    markets, coefs, _ = characteristics.shape
    cores, chips = lax.axis_size("prod"), lax.axis_size("draw")
    own_markets = markets // (cores * chips)
    core, chip = lax.axis_index("prod"), lax.axis_index("draw")

    half = lax.dynamic_slice_in_dim(taste_draws, core * (markets // cores), markets // cores, 0)
    taste = lax.all_to_all(half.reshape(chips, own_markets, coefs, LANES), "draw", 0, 0, tiled=True)

    def packed(first):
        chars = lax.dynamic_slice_in_dim(characteristics, first, own_markets, 0).reshape(-1, LANES)
        utility = lax.dynamic_slice_in_dim(start_utility, first, own_markets, 0)
        shares = lax.dynamic_slice_in_dim(log_shares, first, own_markets, 0)
        return jnp.concatenate([chars, utility, shares], axis=0)

    place = chip * own_markets
    own = packed(core * (markets // cores) + place)
    other = lax.ppermute(packed((1 - core) * (markets // cores) + place), "prod", [(0, 1), (1, 0)])

    blocks = contraction(core.reshape(1), coef_scale, own, other, taste)
    blocks = lax.all_to_all(blocks, ("prod", "draw"), 0, 0, tiled=True)
    utility = blocks[:, :own_markets].reshape(markets, LANES)
    squares = jnp.sum(blocks[:, own_markets : own_markets + 2], axis=0)
    planes = lax.axis_size("mkt")
    step = 1
    while step < planes:
        squares = squares + lax.ppermute(squares, "mkt", [(i, i ^ step) for i in range(planes)])
        step *= 2
    cells = planes * markets * cores * LANES
    return utility, jnp.sqrt(jnp.sum(squares, axis=1) / cells + 1e-06)


def solution(mesh):
    return jax.shard_map(
        shards,
        mesh=mesh,
        in_specs=(
            P("mkt", "prod"),
            P("mkt", "prod"),
            P("mkt", None, "prod"),
            P(),
            P("mkt", None, "draw"),
        ),
        out_specs=(P("mkt", "prod"), P()),
        check_vma=False,
    )
```

time: 203 us -> 60 us (0.30)
  the two profiles are of different devices: /device:TPU:1 before, /device:TPU:32 now
where the time goes in v1:
time: 60 us; the launch traced here: 59.6 us
  starting transfers between devices  16.5 us (28%)
  waiting for transfers between devices  15.8 us (26%)
  blocking collectives  12.4 us (21%)
  Pallas kernels  9.34 us (16%)
  local copies, waits for them, and re-layouts  4.24 us (7%)
  between operations  0.71 us (1%)
  other arithmetic  0.7 us (1%)
    all_to_all x1, blocking collectives, shards(): blocks = lax.all_to_all(blocks, ('prod', 'draw'), 0, 0, tiled=True)  12.4 us
    ppermute x3, starting transfers between devices, shards(): lax.ppermute(squares, 'mkt', [(i, i ^ step) for i in range(planes)])  9.38 us
    pallas_call x1, Pallas kernels, contraction(): pl.pallas_call(contraction_kernel, out_shape=jax.ShapeDtypeStruct((2 * ch...  9.34 us
    all_to_all x1, waiting for transfers between devices, shards(): lax.all_to_all(half.reshape(chips, own_markets, coefs, LANES), 'draw', 0,...  8.68 us
    all_to_all x1, starting transfers between devices, shards(): lax.all_to_all(half.reshape(chips, own_markets, coefs, LANES), 'draw', 0,...  7.03 us
    ppermute x3, waiting for transfers between devices, shards(): lax.ppermute(squares, 'mkt', [(i, i ^ step) for i in range(planes)])  5.91 us
    unnamed x4, local copies, waits for them, and re-layouts  1.22 us
  transfers between devices with their start and end apart: 5, of which 5 were waited for; matrix products, arithmetic and copies ran while one was open for 4% of the time, Pallas kernels for 0%

profile of v1, /device:TPU:32, one launch (start us, length us, event | category | flops | bytes accessed | tf_op | source)
XLA Modules:
  0.0 59.6 jit_solution(14079140466496830387)
XLA Ops:
  0.6 0.0 copy-start
  0.7 1.2 %copy-done = f32[256,8,128]{2,1,0:T(8,128)S(1)} copy-done((f32[256,8,128]{2,1,0:T(8,128)S(1)}, f32[256,8,128]{2,1,0:T(8,128)}, u32[]{:S(2)}) %copy-start) | copy-done | bytes 1048600
  1.9 0.8 %constant_dynamic-slice_fusion = f32[128,8,128]{2,1,0:T(8,128)} fusion(f32[256,8,128]{2,1,0:T(8,128)S(1)} %copy-done, s32[]{:T(128)S(6)} %select_n.15), kind=kLoop, calls=%fused_computation.6 | loop fusion | bytes 1048580 | tf_op jit(solution)/shard_map/dynamic_slice | solution.py:158
  2.7 7.0 %all-to-all-start = ((f32[16,8,8,128]{3,2,1,0:T(8,128)}), f32[16,8,8,128]{3,2,1,0:T(8,128)S(1)}, u32[]{:S(2)}, u32[]{:S(2)}) async-start(f32[16,8,8,128]{3,2,1,0:T(8,128)} %bitcast.3), calls=%async_computation | async-start | bytes 1048576 | tf_op jit(solution)/shard_map/all_to_all | solution.py:159
  9.7 0.7 %constant_dynamic-slice_fusion.1 = (f32[8,128]{1,0:T(8,128)S(1)}, f32[8,128]{1,0:T(8,128)S(1)}, f32[8,128]{1,0:T(8,128)S(1)}, f32[8,128]{1,0:T(8,128)S(1)}) fusion(f32[256,128]{1,0:T(8,128)} %param.6, s32[]{:T(128)S(6)} %select_n.14, s32[]{:T(128)S(6)} %select_n.6, f32[256,128]{1,0:T(8,128)} %param.5), kind=kLoop, calls=%fused_computation.7 | loop fusion | bytes 32776 | tf_op jit(solution)/shard_map/dynamic_slice | solution.py:164
  10.5 0.8 %dynamic-slice_bitcast_fusion = (f32[64,128]{1,0:T(8,128)S(1)}, f32[64,128]{1,0:T(8,128)S(1)}) fusion(f32[256,8,128]{2,1,0:T(8,128)} %param.7, s32[]{:T(128)S(6)} %select_n.14, s32[]{:T(128)S(6)} %select_n.6), kind=kLoop, calls=%fused_computation.4 | loop fusion | bytes 131080 | tf_op jit(solution)/shard_map/reshape | solution.py:162
  11.3 0.1 collective-permute-start
  11.4 0.0 copy-start.1
  11.4 1.2 %collective-permute-done.other_ref = f32[80,128]{1,0:T(8,128)S(1)} collective-permute-done((f32[80,128]{1,0:T(8,128)S(1)}, f32[80,128]{1,0:T(8,128)S(1)}, u32[]{:S(2)}, u32[]{:S(2)}) %collective-permute-start) | collective-permute-done | bytes 40992 | tf_op jit(solution)/shard_map/ppermute | solution.py:169
  12.6 8.7 %all-to-all-done.taste_ref = f32[16,8,8,128]{3,2,1,0:T(8,128)S(1)} async-done(((f32[16,8,8,128]{3,2,1,0:T(8,128)}), f32[16,8,8,128]{3,2,1,0:T(8,128)S(1)}, u32[]{:S(2)}, u32[]{:S(2)}) %all-to-all-start) | async-done | bytes 524320 | tf_op jit(solution)/shard_map/all_to_all | solution.py:159
  21.3 0.0 copy-done.1
  21.3 9.3 %shard_map.68 = f32[32,16,128]{2,1,0:T(8,128)S(1)} custom-call(s32[1]{0:T(128)} %bitcast.core_ref, f32[8]{0:T(128)S(1)} %copy-done.1, f32[80,128]{1,0:T(8,128)S(1)} %pad_maximum_fusion.own_ref, f32[80,128]{1,0:T(8,128)S(1)} %collective-permute-done.other_ref, f32[16,8,8,128]{3,2,1,0:T(8,128)S(1)} %all-to-all-done.taste_ref), custom_call_target="tpu_custom_call" | custom-call | tf_op jit(solution)/shard_map/pallas_call | solution.py:137
  30.6 12.4 %all_to_all.10 = f32[32,16,128]{2,1,0:T(8,128)S(1)} all-to-all(f32[32,16,128]{2,1,0:T(8,128)S(1)} %shard_map.68), channel_id=1, replica_groups=mesh['mkt'=8,'prod'=2,'draw'=16] {'prod','draw'}, dimensions={0} | all-to-all | bytes 524288 | tf_op jit(solution)/shard_map/all_to_all | solution.py:172
  43.0 0.2 collective-permute-start.1
  43.2 3.5 %collective-permute-done.1 = f32[2,128]{1,0:T(2,128)S(1)} collective-permute-done((f32[2,128]{1,0:T(2,128)S(1)}, f32[2,128]{1,0:T(2,128)S(1)}, u32[]{:S(2)}, u32[]{:S(2)}) %collective-permute-start.1) | collective-permute-done | bytes 1056 | tf_op jit(solution)/shard_map/ppermute | solution.py:178
  46.7 3.3 %collective-permute-start.2 = (f32[2,128]{1,0:T(2,128)S(1)}, f32[2,128]{1,0:T(2,128)S(1)}, u32[]{:S(2)}, u32[]{:S(2)}) collective-permute-start(f32[2,128]{1,0:T(2,128)S(1)} %add.36), channel_id=1, source_target_pairs={{0,64},{32,96},{64,0},{96,32},{128,192},{160,224},{192,128},{224,1... | collective-permute-start | bytes 3080 | tf_op jit(solution)/shard_map/ppermute | solution.py:178
  49.9 1.6 %collective-permute-done.2 = f32[2,128]{1,0:T(2,128)S(1)} collective-permute-done((f32[2,128]{1,0:T(2,128)S(1)}, f32[2,128]{1,0:T(2,128)S(1)}, u32[]{:S(2)}, u32[]{:S(2)}) %collective-permute-start.2) | collective-permute-done | bytes 1056 | tf_op jit(solution)/shard_map/ppermute | solution.py:178
  51.5 5.9 %collective-permute-start.3 = (f32[2,128]{1,0:T(2,128)S(1)}, f32[2,128]{1,0:T(2,128)S(1)}, u32[]{:S(2)}, u32[]{:S(2)}) collective-permute-start(f32[2,128]{1,0:T(2,128)S(1)} %add.37), channel_id=1, source_target_pairs={{0,128},{32,160},{64,192},{96,224},{128,0},{160,32},{192,64},{224,... | collective-permute-start | bytes 3080 | tf_op jit(solution)/shard_map/ppermute | solution.py:178
  57.4 0.7 %slice_bitcast_fusion = f32[256,128]{1,0:T(8,128)} fusion(f32[32,16,128]{2,1,0:T(8,128)S(1)} %all_to_all.10), kind=kLoop, calls=%fused_computation | loop fusion | bytes 262144 | tf_op jit(solution)/shard_map/reshape | solution.py:173
  58.1 0.9 %collective-permute-done.3 = f32[2,128]{1,0:T(2,128)S(1)} collective-permute-done((f32[2,128]{1,0:T(2,128)S(1)}, f32[2,128]{1,0:T(2,128)S(1)}, u32[]{:S(2)}, u32[]{:S(2)}) %collective-permute-start.3) | collective-permute-done | bytes 1056 | tf_op jit(solution)/shard_map/ppermute | solution.py:178
  59.0 0.1 add_reduce_fusion
  59.1 0.5 add_sqrt_fusion
  (5 shorter events, 0.1 us)
Async XLA Ops:
  0.6 1.2 %copy-start = (f32[256,8,128]{2,1,0:T(8,128)S(1)}, f32[256,8,128]{2,1,0:T(8,128)}, u32[]{:S(2)}) copy-start(f32[256,8,128]{2,1,0:T(8,128)} %param.9) | copy-start | bytes 3145732
  2.7 18.6 %all-to-all-start = ((f32[16,8,8,128]{3,2,1,0:T(8,128)}), f32[16,8,8,128]{3,2,1,0:T(8,128)S(1)}, u32[]{:S(2)}, u32[]{:S(2)}) async-start(f32[16,8,8,128]{3,2,1,0:T(8,128)} %bitcast.3), calls=%async_computation | async-start | bytes 1048576 | tf_op jit(solution)/shard_map/all_to_all | solution.py:159
  11.3 1.3 %collective-permute-start = (f32[80,128]{1,0:T(8,128)S(1)}, f32[80,128]{1,0:T(8,128)S(1)}, u32[]{:S(2)}, u32[]{:S(2)}) collective-permute-start(f32[80,128]{1,0:T(8,128)S(1)} %pad_maximum_fusion.1), channel_id=1, source_target_pairs={{0,16},{16,0},{1,17},{17,1},{2,18},{18,2},{3,19},{19,3},{4,20},{20... | collective-permute-start | bytes 122888 | tf_op jit(solution)/shard_map/ppermute | solution.py:169
  11.4 9.9 %copy-start.1 = (f32[8]{0:T(128)S(1)}, f32[8]{0:T(128)}, u32[]{:S(2)}) copy-start(f32[8]{0:T(128)} %coef_ref.1) | copy-start | bytes 100
  43.0 3.7 %collective-permute-start.1 = (f32[2,128]{1,0:T(2,128)S(1)}, f32[2,128]{1,0:T(2,128)S(1)}, u32[]{:S(2)}, u32[]{:S(2)}) collective-permute-start(f32[2,128]{1,0:T(2,128)S(1)} %slice_reduce_fusion), channel_id=1, source_target_pairs={{0,32},{32,0},{64,96},{96,64},{128,160},{160,128},{192,224},{224,1... | collective-permute-start | bytes 3080 | tf_op jit(solution)/shard_map/ppermute | solution.py:178
  46.7 4.8 %collective-permute-start.2 = (f32[2,128]{1,0:T(2,128)S(1)}, f32[2,128]{1,0:T(2,128)S(1)}, u32[]{:S(2)}, u32[]{:S(2)}) collective-permute-start(f32[2,128]{1,0:T(2,128)S(1)} %add.36), channel_id=1, source_target_pairs={{0,64},{32,96},{64,0},{96,32},{128,192},{160,224},{192,128},{224,1... | collective-permute-start | bytes 3080 | tf_op jit(solution)/shard_map/ppermute | solution.py:178
  51.5 7.5 %collective-permute-start.3 = (f32[2,128]{1,0:T(2,128)S(1)}, f32[2,128]{1,0:T(2,128)S(1)}, u32[]{:S(2)}, u32[]{:S(2)}) collective-permute-start(f32[2,128]{1,0:T(2,128)S(1)} %add.37), channel_id=1, source_target_pairs={{0,128},{32,160},{64,192},{96,224},{128,0},{160,32},{192,64},{224,... | collective-permute-start | bytes 3080 | tf_op jit(solution)/shard_map/ppermute | solution.py:178

commit v2 on v1

v2 whole, which is shorter than its diff:
```python
import math

import jax
import jax.numpy as jnp
from jax import lax
from jax.experimental import pallas as pl
from jax.experimental.pallas import tpu as pltpu
from jax.sharding import PartitionSpec as P

R = 2048
LOG2E = math.log2(math.e)
LANES = 128
SUBLANES = 8


def rounded(x):
    return x.astype(jnp.bfloat16).astype(jnp.float32)


def first_rows(rows, length):
    width = rows[0].shape[-1]
    index = lax.broadcasted_iota(jnp.int32, (length, width), 0)
    out = jnp.zeros((length, width), jnp.float32)
    for position, row in enumerate(rows):
        out = jnp.where(index == position, jnp.broadcast_to(row, (length, width)), out)
    return out


def three_parts(x):
    high = rounded(x)
    middle = rounded(x - high)
    return high, middle, x - high - middle


def by_first(a, b):
    return lax.dot_general(a, b, (((0,), (0,)), ((), ())), preferred_element_type=jnp.float32)


def all_sublanes(x):
    for shift in (4, 2, 1):
        x = x + pltpu.roll(x, shift, 0)
    return x


def added(terms):
    while len(terms) > 1:
        terms = [a + b for a, b in zip(terms[::2], terms[1::2])]
    return terms[0]


def contraction_kernel(coef_ref, own_ref, other_ref, taste_ref, out_ref, weight_ref, inverse_ref, share_ref, factor_ref, left_ref, row_ref):
    markets = own_ref.shape[0] // 10
    coefs = 8
    chips = taste_ref.shape[0]
    groups = 2 * LANES // SUBLANES
    slices = chips // 2

    def part(first, count):
        return jnp.concatenate([own_ref[pl.ds(first, count)], other_ref[pl.ds(first, count)]], axis=1)

    coef = jnp.concatenate([jnp.full((1, 2 * LANES), coef_ref[k] * LOG2E, jnp.float32) for k in range(coefs)], axis=0)
    ones = first_rows([jnp.ones((1, 2 * LANES), jnp.float32)] * 3, SUBLANES)

    def left_of(m):
        chars = part(m * coefs, coefs) * coef
        high = rounded(chars)
        base = first_rows(three_parts(part(8 * markets + m, 1) * LOG2E), SUBLANES)
        left_ref[m] = jnp.concatenate([high, high, chars - high, base], axis=0).astype(jnp.bfloat16)

    def weigh(m, q):
        taste = jnp.concatenate([taste_ref[2 * q, m], taste_ref[2 * q + 1, m]], axis=1)
        taste_high = rounded(taste)
        right = jnp.concatenate([taste_high, taste - taste_high, taste_high, ones], axis=0).astype(jnp.bfloat16)
        weight = jnp.exp2(by_first(left_ref[m], right))
        for half in range(2):
            piece = weight[:, half * LANES : (half + 1) * LANES]
            weight_ref[m, 2 * q + half] = piece
            total = jnp.sum(piece.reshape(groups, SUBLANES, LANES), axis=0)
            inverse_ref[m, 2 * q + half] = 1.0 / (1.0 + all_sublanes(total))

    def share(m, q):
        inverse = [inverse_ref[m, t] for t in range(chips)]
        for g in range(q * groups // slices, (q + 1) * groups // slices):
            rows = pl.ds(g * SUBLANES, SUBLANES)
            share_ref[m, rows] = added([weight_ref[m, t, rows] * inverse[t] for t in range(chips)])

    def predicted(m):
        return jnp.sum(share_ref[m].T, axis=0, keepdims=True) * (1.0 / R)

    def first_end(m):
        change = part(9 * markets + m, 1) - jnp.log(predicted(m))
        factor = jnp.exp(change)
        row_ref[0, pl.ds(m, 1)] = change
        row_ref[1, pl.ds(m, 1)] = factor
        factor_ref[m] = jnp.broadcast_to(factor, (LANES, 2 * LANES)).T

    def weigh_again(m, q):
        totals = [[] for _ in range(2)]
        for g in range(groups):
            rows = pl.ds(g * SUBLANES, SUBLANES)
            scale = factor_ref[m, rows]
            for half in range(2):
                term = weight_ref[m, 2 * q + half, rows] * scale
                if g < 2:
                    totals[half].append(term)
                else:
                    totals[half][g % 2] = totals[half][g % 2] + term
        for half in range(2):
            inverse_ref[m, 2 * q + half] = 1.0 / (1.0 + all_sublanes(added(totals[half])))

    def second_end(m):
        row_ref[2, pl.ds(m, 1)] = predicted(m)

    for stage in range(markets + 3):
        a, b, c, d = (stage - lag if 0 <= stage - lag < markets else None for lag in range(4))
        if a is not None:
            left_of(a)
        for q in range(slices):
            if a is not None:
                weigh(a, q)
            if b is not None:
                share(b, q)
            if c is not None:
                weigh_again(c, q)
            if d is not None:
                share(d, q)
        if b is not None:
            first_end(b)
        if d is not None:
            second_end(d)

    first_change = row_ref[0]
    second_change = part(9 * markets, markets) - jnp.log(row_ref[1] * row_ref[2])
    result = part(8 * markets, markets) + first_change + second_change
    squares = []
    for change in (first_change, second_change):
        square = change * change
        square = square[:, :LANES] + square[:, LANES:]
        squares.append(jnp.sum(square, axis=0, keepdims=True))
    block = jnp.concatenate([result[:, :LANES], result[:, LANES:], first_rows(squares, SUBLANES)], axis=0)
    out_ref[...] = jnp.broadcast_to(block, (chips, 3 * SUBLANES, LANES))


def contraction(coef_scale, own, other, taste):
    chips, markets, _, _ = taste.shape
    smem = pl.BlockSpec(memory_space=pltpu.SMEM)
    vmem = pl.BlockSpec(memory_space=pltpu.VMEM)
    return pl.pallas_call(
        contraction_kernel,
        out_shape=jax.ShapeDtypeStruct((chips, 3 * SUBLANES, LANES), jnp.float32),
        in_specs=[smem, vmem, vmem, vmem],
        out_specs=vmem,
        scratch_shapes=[
            pltpu.VMEM((markets, chips, 2 * LANES, LANES), jnp.float32),
            pltpu.VMEM((markets, chips, SUBLANES, LANES), jnp.float32),
            pltpu.VMEM((markets, 2 * LANES, LANES), jnp.float32),
            pltpu.VMEM((markets, 2 * LANES, LANES), jnp.float32),
            pltpu.VMEM((markets, 4 * SUBLANES, 2 * LANES), jnp.bfloat16),
            pltpu.VMEM((3, markets, 2 * LANES), jnp.float32),
        ],
        compiler_params=pltpu.CompilerParams(vmem_limit_bytes=40 * 1024 * 1024),
    )(coef_scale, own, other, taste)


def take_half_kernel(core_ref, whole_ref, half_ref, sem):
    count = half_ref.shape[0]
    copy = pltpu.make_async_copy(whole_ref.at[pl.ds(core_ref[0] * count, count)], half_ref, sem)
    copy.start()
    copy.wait()


def take_half(core, whole, count):
    return pl.pallas_call(
        take_half_kernel,
        out_shape=jax.ShapeDtypeStruct((count, *whole.shape[1:]), whole.dtype),
        in_specs=[pl.BlockSpec(memory_space=pltpu.SMEM), pl.BlockSpec(memory_space=pltpu.HBM)],
        out_specs=pl.BlockSpec(memory_space=pltpu.VMEM),
        scratch_shapes=[pltpu.SemaphoreType.DMA(())],
    )(core.reshape(1), whole)


def shards(start_utility, log_shares, characteristics, coef_scale, taste_draws):
    markets, coefs, _ = characteristics.shape
    cores, chips, planes = lax.axis_size("prod"), lax.axis_size("draw"), lax.axis_size("mkt")
    half = markets // cores
    own_markets = half // chips
    core, chip = lax.axis_index("prod"), lax.axis_index("draw")

    taste = take_half(core, taste_draws, half).reshape(chips, own_markets, coefs, LANES)
    taste = lax.all_to_all(taste, "draw", 0, 0, tiled=True)

    def packed(first):
        chars = lax.dynamic_slice_in_dim(characteristics, first, own_markets, 0).reshape(-1, LANES)
        utility = lax.dynamic_slice_in_dim(start_utility, first, own_markets, 0)
        shares = lax.dynamic_slice_in_dim(log_shares, first, own_markets, 0)
        return jnp.concatenate([chars, utility, shares], axis=0)

    swap = [(0, 1), (1, 0)]
    own = packed(core * half + chip * own_markets)
    other = lax.ppermute(packed((1 - core) * half + chip * own_markets), "prod", swap)

    blocks = contraction(coef_scale, own, other, taste)
    blocks = lax.all_to_all(blocks, "draw", 0, 0, tiled=True)

    squares = jnp.sum(blocks[:, 2 * own_markets : 2 * own_markets + 2], axis=0)
    squares = jnp.broadcast_to(squares, (planes * cores, 2, LANES))
    squares = lax.all_to_all(squares, ("mkt", "prod"), 0, 0, tiled=True)
    kept = blocks[:, :own_markets].reshape(half, LANES)
    given = blocks[:, own_markets : 2 * own_markets].reshape(half, LANES)
    given = lax.ppermute(given, "prod", swap)
    first = core == 0
    utility = jnp.concatenate([jnp.where(first, kept, given), jnp.where(first, given, kept)], axis=0)
    cells = planes * markets * cores * LANES
    return utility, jnp.sqrt(jnp.sum(squares, axis=(0, 2)) / cells + 1e-06)


def solution(mesh):
    return jax.shard_map(
        shards,
        mesh=mesh,
        in_specs=(
            P("mkt", "prod"),
            P("mkt", "prod"),
            P("mkt", None, "prod"),
            P(),
            P("mkt", None, "draw"),
        ),
        out_specs=(P("mkt", "prod"), P()),
        check_vma=False,
    )
```

time: 60 us -> 60 us (level)
  the two profiles are of different devices: /device:TPU:32 before, /device:TPU:1 now
where the time goes in v2:
time: 60 us; the launch traced here: 59.5 us
  starting transfers between devices  24 us (40%)
  waiting for transfers between devices  22.1 us (37%)
  Pallas kernels  9.17 us (15%)
  local copies, waits for them, and re-layouts  2.15 us (4%)
  other arithmetic  1.37 us (2%)
  between operations  0.7 us (1%)
    all_to_all x1, starting transfers between devices, shards(): squares = lax.all_to_all(squares, ('mkt', 'prod'), 0, 0, tiled=True)  11.7 us
    all_to_all x1, starting transfers between devices, shards(): taste = lax.all_to_all(taste, 'draw', 0, 0, tiled=True)  7.58 us
    pallas_call x1, Pallas kernels, contraction(): pl.pallas_call(contraction_kernel, out_shape=jax.ShapeDtypeStruct((chips,...  7.32 us
    all_to_all x1, waiting for transfers between devices, shards(): blocks = lax.all_to_all(blocks, 'draw', 0, 0, tiled=True)  7.15 us
    all_to_all x1, waiting for transfers between devices, shards(): squares = lax.all_to_all(squares, ('mkt', 'prod'), 0, 0, tiled=True)  7.13 us
    all_to_all x1, waiting for transfers between devices, shards(): taste = lax.all_to_all(taste, 'draw', 0, 0, tiled=True)  6.97 us
    all_to_all x1, starting transfers between devices, shards(): blocks = lax.all_to_all(blocks, 'draw', 0, 0, tiled=True)  3.52 us
    pallas_call x1, Pallas kernels, take_half(): pl.pallas_call(take_half_kernel, out_shape=jax.ShapeDtypeStruct((count, *...  1.84 us
  transfers between devices with their start and end apart: 5, of which 4 were waited for; matrix products, arithmetic and copies ran while one was open for 4% of the time, Pallas kernels for 0%

profile of v2, /device:TPU:1, one launch (start us, length us, event | category | flops | bytes accessed | tf_op | source)
XLA Modules:
  0.0 59.5 jit_solution(12160717202625798606)
XLA Ops:
  0.6 1.8 %shard_map.68 = f32[128,8,128]{2,1,0:T(8,128)} custom-call(s32[1]{0:T(128)} %bitcast.2.core_ref, f32[256,8,128]{2,1,0:T(8,128)} %whole_ref.1), custom_call_target="tpu_custom_call" | custom-call | tf_op jit(solution)/shard_map/pallas_call | solution.py:173
  2.5 7.6 %all-to-all-start = ((f32[16,8,8,128]{3,2,1,0:T(8,128)}), f32[16,8,8,128]{3,2,1,0:T(8,128)S(1)}, u32[]{:S(2)}, u32[]{:S(2)}) async-start(f32[16,8,8,128]{3,2,1,0:T(8,128)} %bitcast.14), calls=%async_computation | async-start | bytes 1048576 | tf_op jit(solution)/shard_map/all_to_all | solution.py:190
  10.1 0.7 %constant_dynamic-slice_fusion = (f32[8,128]{1,0:T(8,128)S(1)}, f32[8,128]{1,0:T(8,128)S(1)}, f32[8,128]{1,0:T(8,128)S(1)}, f32[8,128]{1,0:T(8,128)S(1)}) fusion(f32[256,128]{1,0:T(8,128)} %param.6, s32[]{:T(128)S(6)} %select_n.24, s32[]{:T(128)S(6)} %select_n.23, f32[256,128]{1,0:T(8,128)} %param.5), kind=kLoop, calls=%fused_computation.10 | loop fusion | bytes 32776 | tf_op jit(solution)/shard_map/dynamic_slice | solution.py:195
  10.8 0.8 %dynamic-slice_bitcast_fusion = (f32[64,128]{1,0:T(8,128)S(1)}, f32[64,128]{1,0:T(8,128)S(1)}) fusion(f32[256,8,128]{2,1,0:T(8,128)} %param.7, s32[]{:T(128)S(6)} %select_n.24, s32[]{:T(128)S(6)} %select_n.23), kind=kLoop, calls=%fused_computation.7 | loop fusion | bytes 131080 | tf_op jit(solution)/shard_map/reshape | solution.py:193
  11.6 1.0 %collective-permute-start = (f32[80,128]{1,0:T(8,128)S(1)}, f32[80,128]{1,0:T(8,128)S(1)}, u32[]{:S(2)}, u32[]{:S(2)}) collective-permute-start(f32[80,128]{1,0:T(8,128)S(1)} %pad_maximum_fusion.2), channel_id=1, source_target_pairs={{0,16},{16,0},{1,17},{17,1},{2,18},{18,2},{3,19},{19,3},{4,20},{20... | collective-permute-start | bytes 122888 | tf_op jit(solution)/shard_map/ppermute | solution.py:200
  12.7 0.0 copy-start
  12.7 0.9 %collective-permute-done.other_ref = f32[80,128]{1,0:T(8,128)S(1)} collective-permute-done((f32[80,128]{1,0:T(8,128)S(1)}, f32[80,128]{1,0:T(8,128)S(1)}, u32[]{:S(2)}, u32[]{:S(2)}) %collective-permute-start) | collective-permute-done | bytes 40992 | tf_op jit(solution)/shard_map/ppermute | solution.py:200
  13.5 7.0 %all-to-all-done.taste_ref = f32[16,8,8,128]{3,2,1,0:T(8,128)S(1)} async-done(((f32[16,8,8,128]{3,2,1,0:T(8,128)}), f32[16,8,8,128]{3,2,1,0:T(8,128)S(1)}, u32[]{:S(2)}, u32[]{:S(2)}) %all-to-all-start) | async-done | bytes 524320 | tf_op jit(solution)/shard_map/all_to_all | solution.py:190
  20.5 0.0 copy-done
  20.5 7.3 %shard_map.69 = f32[16,24,128]{2,1,0:T(8,128)} custom-call(f32[8]{0:T(128)S(1)} %copy-done, f32[80,128]{1,0:T(8,128)S(1)} %pad_maximum_fusion.1.own_ref, f32[80,128]{1,0:T(8,128)S(1)} %collective-permute-done.other_ref, f32[16,8,8,128]{3,2,1,0:T(8,128)S(1)} %all-to-all-done.taste_ref), custom_call_target="tpu_custom_call" | custom-call | tf_op jit(solution)/shard_map/pallas_call | solution.py:148
  27.8 3.5 %all-to-all-start.1 = ((f32[16,24,128]{2,1,0:T(8,128)}), f32[16,24,128]{2,1,0:T(8,128)S(1)}, u32[]{:S(2)}, u32[]{:S(2)}) async-start(f32[16,24,128]{2,1,0:T(8,128)} %shard_map.69), calls=%async_computation.1 | async-start | bytes 393216 | tf_op jit(solution)/shard_map/all_to_all | solution.py:203
  31.4 7.1 %all-to-all-done.1 = f32[16,24,128]{2,1,0:T(8,128)S(1)} async-done(((f32[16,24,128]{2,1,0:T(8,128)}), f32[16,24,128]{2,1,0:T(8,128)S(1)}, u32[]{:S(2)}, u32[]{:S(2)}) %all-to-all-start.1) | async-done | bytes 196640 | tf_op jit(solution)/shard_map/all_to_all | solution.py:203
  38.5 0.6 %broadcast_in_dim.3 = f32[16,2,128]{2,1,0:T(2,128)} broadcast(f32[2,128]{1,0:T(2,128)S(1)} %slice_reduce_fusion), dimensions={1,2} | broadcast | bytes 17408 | tf_op jit(solution)/shard_map/broadcast_in_dim | solution.py:206
  39.1 11.7 %all-to-all-start.2 = ((f32[16,2,128]{2,1,0:T(2,128)}), f32[16,2,128]{2,1,0:T(2,128)S(1)}, u32[]{:S(2)}, u32[]{:S(2)}) async-start(f32[16,2,128]{2,1,0:T(2,128)} %broadcast_in_dim.3), calls=%async_computation.2 | async-start | bytes 32768 | tf_op jit(solution)/shard_map/all_to_all | solution.py:207
  50.8 0.2 collective-permute-start.1
  51.0 7.1 %all-to-all-done.2 = f32[16,2,128]{2,1,0:T(2,128)S(1)} async-done(((f32[16,2,128]{2,1,0:T(2,128)}), f32[16,2,128]{2,1,0:T(2,128)S(1)}, u32[]{:S(2)}, u32[]{:S(2)}) %all-to-all-start.2) | async-done | bytes 16416 | tf_op jit(solution)/shard_map/all_to_all | solution.py:207
  58.2 0.1 reduce_sum.19
  58.3 0.5 add_sqrt_fusion
  58.8 0.0 collective-permute-done.1
  58.9 0.7 %pad_maximum_fusion = f32[256,128]{1,0:T(8,128)} fusion(f32[128,128]{1,0:T(8,128)S(1)} %get-tuple-element.5, f32[128,128]{1,0:T(8,128)S(1)} %get-tuple-element.4), kind=kLoop, calls=%fused_computation | loop fusion | flops 32768 | bytes 262144 | tf_op jit(solution)/shard_map/concatenate | solution.py:212
  (5 shorter events, 0.0 us)
Async XLA Ops:
  2.5 18.0 %all-to-all-start = ((f32[16,8,8,128]{3,2,1,0:T(8,128)}), f32[16,8,8,128]{3,2,1,0:T(8,128)S(1)}, u32[]{:S(2)}, u32[]{:S(2)}) async-start(f32[16,8,8,128]{3,2,1,0:T(8,128)} %bitcast.14), calls=%async_computation | async-start | bytes 1048576 | tf_op jit(solution)/shard_map/all_to_all | solution.py:190
  11.6 1.9 %collective-permute-start = (f32[80,128]{1,0:T(8,128)S(1)}, f32[80,128]{1,0:T(8,128)S(1)}, u32[]{:S(2)}, u32[]{:S(2)}) collective-permute-start(f32[80,128]{1,0:T(8,128)S(1)} %pad_maximum_fusion.2), channel_id=1, source_target_pairs={{0,16},{16,0},{1,17},{17,1},{2,18},{18,2},{3,19},{19,3},{4,20},{20... | collective-permute-start | bytes 122888 | tf_op jit(solution)/shard_map/ppermute | solution.py:200
  12.7 7.8 %copy-start = (f32[8]{0:T(128)S(1)}, f32[8]{0:T(128)}, u32[]{:S(2)}) copy-start(f32[8]{0:T(128)} %coef_ref.1) | copy-start | bytes 100
  27.8 10.7 %all-to-all-start.1 = ((f32[16,24,128]{2,1,0:T(8,128)}), f32[16,24,128]{2,1,0:T(8,128)S(1)}, u32[]{:S(2)}, u32[]{:S(2)}) async-start(f32[16,24,128]{2,1,0:T(8,128)} %shard_map.69), calls=%async_computation.1 | async-start | bytes 393216 | tf_op jit(solution)/shard_map/all_to_all | solution.py:203
  39.1 19.0 %all-to-all-start.2 = ((f32[16,2,128]{2,1,0:T(2,128)}), f32[16,2,128]{2,1,0:T(2,128)S(1)}, u32[]{:S(2)}, u32[]{:S(2)}) async-start(f32[16,2,128]{2,1,0:T(2,128)} %broadcast_in_dim.3), calls=%async_computation.2 | async-start | bytes 32768 | tf_op jit(solution)/shard_map/all_to_all | solution.py:207
  50.8 8.0 %collective-permute-start.1 = (f32[128,128]{1,0:T(8,128)S(1)}, f32[128,128]{1,0:T(8,128)S(1)}, u32[]{:S(2)}, u32[]{:S(2)}) collective-permute-start(f32[128,128]{1,0:T(8,128)S(1)} %slice_bitcast_fusion), channel_id=1, source_target_pairs={{0,16},{16,0},{1,17},{17,1},{2,18},{18,2},{3,19},{19,3},{4,20},{20... | collective-permute-start | bytes 196616 | tf_op jit(solution)/shard_map/ppermute | solution.py:210

commit v3 on v2

--- a/solution.py
+++ b/solution.py
@@ -94,19 +94,19 @@
         row_ref[1, pl.ds(m, 1)] = factor
         factor_ref[m] = jnp.broadcast_to(factor, (LANES, 2 * LANES)).T
 
+    again = {}
+
     def weigh_again(m, q):
-        totals = [[] for _ in range(2)]
-        for g in range(groups):
+        totals = again.setdefault(m, [None] * chips)
+        for g in range(q * groups // slices, (q + 1) * groups // slices):
             rows = pl.ds(g * SUBLANES, SUBLANES)
             scale = factor_ref[m, rows]
-            for half in range(2):
-                term = weight_ref[m, 2 * q + half, rows] * scale
-                if g < 2:
-                    totals[half].append(term)
-                else:
-                    totals[half][g % 2] = totals[half][g % 2] + term
-        for half in range(2):
-            inverse_ref[m, 2 * q + half] = 1.0 / (1.0 + all_sublanes(added(totals[half])))
+            for t in range(chips):
+                term = weight_ref[m, t, rows] * scale
+                totals[t] = term if totals[t] is None else totals[t] + term
+        if q == slices - 1:
+            for t in range(chips):
+                inverse_ref[m, t] = 1.0 / (1.0 + all_sublanes(totals[t]))
 
     def second_end(m):
         row_ref[2, pl.ds(m, 1)] = predicted(m)
@@ -174,9 +174,9 @@
         take_half_kernel,
         out_shape=jax.ShapeDtypeStruct((count, *whole.shape[1:]), whole.dtype),
         in_specs=[pl.BlockSpec(memory_space=pltpu.SMEM), pl.BlockSpec(memory_space=pltpu.HBM)],
-        out_specs=pl.BlockSpec(memory_space=pltpu.VMEM),
+        out_specs=pl.BlockSpec(memory_space=pltpu.HBM),
         scratch_shapes=[pltpu.SemaphoreType.DMA(())],
-    )(core.reshape(1), whole)
+    )(core.astype(jnp.int32).reshape(1), whole)
 
 
 def shards(start_utility, log_shares, characteristics, coef_scale, taste_draws):
@@ -184,7 +184,7 @@
     cores, chips, planes = lax.axis_size("prod"), lax.axis_size("draw"), lax.axis_size("mkt")
     half = markets // cores
     own_markets = half // chips
-    core, chip = lax.axis_index("prod"), lax.axis_index("draw")
+    core, chip = (lax.axis_index(axis).astype(jnp.uint32) for axis in ("prod", "draw"))
 
     taste = take_half(core, taste_draws, half).reshape(chips, own_markets, coefs, LANES)
     taste = lax.all_to_all(taste, "draw", 0, 0, tiled=True)
@@ -208,8 +208,9 @@
     kept = blocks[:, :own_markets].reshape(half, LANES)
     given = blocks[:, own_markets : 2 * own_markets].reshape(half, LANES)
     given = lax.ppermute(given, "prod", swap)
-    first = core == 0
-    utility = jnp.concatenate([jnp.where(first, kept, given), jnp.where(first, given, kept)], axis=0)
+    utility = jnp.zeros((markets, LANES), jnp.float32)
+    utility = lax.dynamic_update_slice_in_dim(utility, kept, core * half, 0)
+    utility = lax.dynamic_update_slice_in_dim(utility, given, (1 - core) * half, 0)
     cells = planes * markets * cores * LANES
     return utility, jnp.sqrt(jnp.sum(squares, axis=(0, 2)) / cells + 1e-06)
 

time: 60 us -> 73.9 us (1.23)
  Pallas kernels: 9.17 us -> 23.6 us
  blocking collectives: 0 us -> 10.5 us
  waiting for transfers between devices: 22.1 us -> 15.1 us
  starting transfers between devices: 24 us -> 20.1 us
    pallas_call x1, Pallas kernels: 1.84 us -> 17 us  [take_half(): pl.pallas_call(take_half_kernel, out_shape=jax.ShapeDtypeStruct((count, *...]
    all_to_all x0 -> x1, blocking collectives: none -> 10.5 us  [shards(): blocks = lax.all_to_all(blocks, 'draw', 0, 0, tiled=True)]
    all_to_all x1 -> x0, waiting for transfers between devices: 7.15 us -> none  [shards(): blocks = lax.all_to_all(blocks, 'draw', 0, 0, tiled=True)]
    all_to_all x1 -> x0, starting transfers between devices: 3.52 us -> none  [shards(): blocks = lax.all_to_all(blocks, 'draw', 0, 0, tiled=True)]
    all_to_all x1, starting transfers between devices: 11.7 us -> 8.59 us  [shards(): squares = lax.all_to_all(squares, ('mkt', 'prod'), 0, 0, tiled=True)]
    ppermute x1, starting transfers between devices: 0.19 us -> 2.89 us  [shards(): given = lax.ppermute(given, 'prod', swap)]
    pallas_call x1, Pallas kernels: 7.32 us -> 6.58 us  [contraction(): pl.pallas_call(contraction_kernel, out_shape=jax.ShapeDtypeStruct((chips,...]
  transfers between devices with their start and end apart: 5 -> 4, of which waited for: 4 -> 3; matrix products, arithmetic and copies ran while one was open for 4% -> 4% of each run, Pallas kernels for 0% -> 0%
where the time goes in v3:
time: 73.9 us; the launch traced here: 73.5 us
  Pallas kernels  23.6 us (32%)
  starting transfers between devices  20.1 us (27%)
  waiting for transfers between devices  15.1 us (20%)
  blocking collectives  10.5 us (14%)
  local copies, waits for them, and re-layouts  2.82 us (4%)
    pallas_call x1, Pallas kernels, take_half(): pl.pallas_call(take_half_kernel, out_shape=jax.ShapeDtypeStruct((count, *...  17 us
    all_to_all x1, blocking collectives, shards(): blocks = lax.all_to_all(blocks, 'draw', 0, 0, tiled=True)  10.5 us
    all_to_all x1, starting transfers between devices, shards(): squares = lax.all_to_all(squares, ('mkt', 'prod'), 0, 0, tiled=True)  8.59 us
    all_to_all x1, starting transfers between devices, shards(): taste = lax.all_to_all(taste, 'draw', 0, 0, tiled=True)  7.58 us
    all_to_all x1, waiting for transfers between devices, shards(): squares = lax.all_to_all(squares, ('mkt', 'prod'), 0, 0, tiled=True)  7.3 us
    all_to_all x1, waiting for transfers between devices, shards(): taste = lax.all_to_all(taste, 'draw', 0, 0, tiled=True)  6.97 us
    pallas_call x1, Pallas kernels, contraction(): pl.pallas_call(contraction_kernel, out_shape=jax.ShapeDtypeStruct((chips,...  6.58 us
    ppermute x1, starting transfers between devices, shards(): given = lax.ppermute(given, 'prod', swap)  2.89 us
  transfers between devices with their start and end apart: 4, of which 3 were waited for; matrix products, arithmetic and copies ran while one was open for 4% of the time, Pallas kernels for 0%

profile of v3, /device:TPU:1, one launch (start us, length us, event | category | flops | bytes accessed | tf_op | source)
XLA Modules:
  0.0 73.5 jit_solution(605300646149860104)
XLA Ops:
  0.6 17.0 %shard_map.68 = f32[128,8,128]{2,1,0:T(8,128)} custom-call(s32[1]{0:T(128)} %bitcast.2.core_ref, f32[256,8,128]{2,1,0:T(8,128)} %whole_ref.1), custom_call_target="tpu_custom_call" | custom-call | tf_op jit(solution)/shard_map/pallas_call | solution.py:173
  17.6 7.6 %all-to-all-start = ((f32[16,8,8,128]{3,2,1,0:T(8,128)}), f32[16,8,8,128]{3,2,1,0:T(8,128)S(1)}, u32[]{:S(2)}, u32[]{:S(2)}) async-start(f32[16,8,8,128]{3,2,1,0:T(8,128)} %bitcast.12), calls=%async_computation | async-start | bytes 1048576 | tf_op jit(solution)/shard_map/all_to_all | solution.py:190
  25.2 0.7 %constant_dynamic-slice_fusion = (f32[8,128]{1,0:T(8,128)S(1)}, f32[8,128]{1,0:T(8,128)S(1)}, f32[8,128]{1,0:T(8,128)S(1)}, f32[8,128]{1,0:T(8,128)S(1)}) fusion(f32[256,128]{1,0:T(8,128)} %param.6, u32[]{:T(128)S(6)} %add.10, u32[]{:T(128)S(6)} %add.9, f32[256,128]{1,0:T(8,128)} %param.5), kind=kLoop, calls=%fused_computation.9 | loop fusion | bytes 32776 | tf_op jit(solution)/shard_map/dynamic_slice | solution.py:195
  26.0 0.8 %dynamic-slice_bitcast_fusion = (f32[64,128]{1,0:T(8,128)S(1)}, f32[64,128]{1,0:T(8,128)S(1)}) fusion(f32[256,8,128]{2,1,0:T(8,128)} %param.7, u32[]{:T(128)S(6)} %add.10, u32[]{:T(128)S(6)} %add.9), kind=kLoop, calls=%fused_computation.5 | loop fusion | bytes 131080 | tf_op jit(solution)/shard_map/reshape | solution.py:193
  26.8 1.0 %collective-permute-start = (f32[80,128]{1,0:T(8,128)S(1)}, f32[80,128]{1,0:T(8,128)S(1)}, u32[]{:S(2)}, u32[]{:S(2)}) collective-permute-start(f32[80,128]{1,0:T(8,128)S(1)} %pad_maximum_fusion.1), channel_id=1, source_target_pairs={{0,16},{16,0},{1,17},{17,1},{2,18},{18,2},{3,19},{19,3},{4,20},{20... | collective-permute-start | bytes 122888 | tf_op jit(solution)/shard_map/ppermute | solution.py:200
  27.8 0.0 copy-start
  27.8 0.9 %collective-permute-done.other_ref = f32[80,128]{1,0:T(8,128)S(1)} collective-permute-done((f32[80,128]{1,0:T(8,128)S(1)}, f32[80,128]{1,0:T(8,128)S(1)}, u32[]{:S(2)}, u32[]{:S(2)}) %collective-permute-start) | collective-permute-done | bytes 40992 | tf_op jit(solution)/shard_map/ppermute | solution.py:200
  28.7 7.0 %all-to-all-done.taste_ref = f32[16,8,8,128]{3,2,1,0:T(8,128)S(1)} async-done(((f32[16,8,8,128]{3,2,1,0:T(8,128)}), f32[16,8,8,128]{3,2,1,0:T(8,128)S(1)}, u32[]{:S(2)}, u32[]{:S(2)}) %all-to-all-start) | async-done | bytes 524320 | tf_op jit(solution)/shard_map/all_to_all | solution.py:190
  35.7 0.0 copy-done
  35.7 6.6 %shard_map.69 = f32[16,24,128]{2,1,0:T(8,128)S(1)} custom-call(f32[8]{0:T(128)S(1)} %copy-done, f32[80,128]{1,0:T(8,128)S(1)} %pad_maximum_fusion.own_ref, f32[80,128]{1,0:T(8,128)S(1)} %collective-permute-done.other_ref, f32[16,8,8,128]{3,2,1,0:T(8,128)S(1)} %all-to-all-done.taste_ref), custom_call_target="tpu_custom_call" | custom-call | tf_op jit(solution)/shard_map/pallas_call | solution.py:148
  42.2 10.5 %all_to_all.15 = f32[16,24,128]{2,1,0:T(8,128)S(1)} all-to-all(f32[16,24,128]{2,1,0:T(8,128)S(1)} %shard_map.69), channel_id=1, replica_groups=mesh['mkt'=8,'prod'=2,'draw'=16] {'draw'}, dimensions={0} | all-to-all | bytes 393216 | tf_op jit(solution)/shard_map/all_to_all | solution.py:203
  52.7 2.9 %collective-permute-start.1 = (f32[128,128]{1,0:T(8,128)S(1)}, f32[128,128]{1,0:T(8,128)S(1)}, u32[]{:S(2)}, u32[]{:S(2)}) collective-permute-start(f32[128,128]{1,0:T(8,128)S(1)} %slice_bitcast_fusion), channel_id=1, source_target_pairs={{0,16},{16,0},{1,17},{17,1},{2,18},{18,2},{3,19},{19,3},{4,20},{20... | collective-permute-start | bytes 196616 | tf_op jit(solution)/shard_map/ppermute | solution.py:210
  55.6 0.6 broadcast_in_dim.7
  56.2 8.6 %all-to-all-start.2 = ((f32[16,2,128]{2,1,0:T(2,128)}), f32[16,2,128]{2,1,0:T(2,128)S(1)}, u32[]{:S(2)}, u32[]{:S(2)}) async-start(f32[16,2,128]{2,1,0:T(2,128)} %broadcast_in_dim.7), calls=%async_computation.2 | async-start | bytes 32768 | tf_op jit(solution)/shard_map/all_to_all | solution.py:207
  64.9 7.3 %all-to-all-done.2 = f32[16,2,128]{2,1,0:T(2,128)S(1)} async-done(((f32[16,2,128]{2,1,0:T(2,128)}), f32[16,2,128]{2,1,0:T(2,128)S(1)}, u32[]{:S(2)}, u32[]{:S(2)}) %all-to-all-start.2) | async-done | bytes 16416 | tf_op jit(solution)/shard_map/all_to_all | solution.py:207
  72.2 0.1 reduce_sum.19
  72.3 0.5 add_sqrt_fusion
  72.8 0.0 collective-permute-done.1
  72.8 0.0 copy-start.1
  72.9 0.6 copy-done.1
  (7 shorter events, 0.1 us)
Async XLA Ops:
  17.6 18.0 %all-to-all-start = ((f32[16,8,8,128]{3,2,1,0:T(8,128)}), f32[16,8,8,128]{3,2,1,0:T(8,128)S(1)}, u32[]{:S(2)}, u32[]{:S(2)}) async-start(f32[16,8,8,128]{3,2,1,0:T(8,128)} %bitcast.12), calls=%async_computation | async-start | bytes 1048576 | tf_op jit(solution)/shard_map/all_to_all | solution.py:190
  26.8 1.9 %collective-permute-start = (f32[80,128]{1,0:T(8,128)S(1)}, f32[80,128]{1,0:T(8,128)S(1)}, u32[]{:S(2)}, u32[]{:S(2)}) collective-permute-start(f32[80,128]{1,0:T(8,128)S(1)} %pad_maximum_fusion.1), channel_id=1, source_target_pairs={{0,16},{16,0},{1,17},{17,1},{2,18},{18,2},{3,19},{19,3},{4,20},{20... | collective-permute-start | bytes 122888 | tf_op jit(solution)/shard_map/ppermute | solution.py:200
  27.8 7.8 %copy-start = (f32[8]{0:T(128)S(1)}, f32[8]{0:T(128)}, u32[]{:S(2)}) copy-start(f32[8]{0:T(128)} %coef_ref.1) | copy-start | bytes 100
  52.7 20.1 %collective-permute-start.1 = (f32[128,128]{1,0:T(8,128)S(1)}, f32[128,128]{1,0:T(8,128)S(1)}, u32[]{:S(2)}, u32[]{:S(2)}) collective-permute-start(f32[128,128]{1,0:T(8,128)S(1)} %slice_bitcast_fusion), channel_id=1, source_target_pairs={{0,16},{16,0},{1,17},{17,1},{2,18},{18,2},{3,19},{19,3},{4,20},{20... | collective-permute-start | bytes 196616 | tf_op jit(solution)/shard_map/ppermute | solution.py:210
  56.2 15.9 %all-to-all-start.2 = ((f32[16,2,128]{2,1,0:T(2,128)}), f32[16,2,128]{2,1,0:T(2,128)S(1)}, u32[]{:S(2)}, u32[]{:S(2)}) async-start(f32[16,2,128]{2,1,0:T(2,128)} %broadcast_in_dim.7), calls=%async_computation.2 | async-start | bytes 32768 | tf_op jit(solution)/shard_map/all_to_all | solution.py:207
  72.8 0.7 copy-start.1

commit v4 on v3

--- a/solution.py
+++ b/solution.py
@@ -48,9 +48,9 @@
     return terms[0]
 
 
-def contraction_kernel(coef_ref, own_ref, other_ref, taste_ref, out_ref, weight_ref, inverse_ref, share_ref, factor_ref, left_ref, row_ref):
-    markets = own_ref.shape[0] // 10
+def contraction_kernel(own_ref, other_ref, taste_ref, out_ref, weight_ref, inverse_ref, share_ref, factor_ref, left_ref, row_ref):
     coefs = 8
+    markets = other_ref.shape[0] // (coefs + 2)
     chips = taste_ref.shape[0]
     groups = 2 * LANES // SUBLANES
     slices = chips // 2
@@ -58,7 +58,8 @@
     def part(first, count):
         return jnp.concatenate([own_ref[pl.ds(first, count)], other_ref[pl.ds(first, count)]], axis=1)
 
-    coef = jnp.concatenate([jnp.full((1, 2 * LANES), coef_ref[k] * LOG2E, jnp.float32) for k in range(coefs)], axis=0)
+    coef = own_ref[pl.ds((coefs + 2) * markets, coefs)] * LOG2E
+    coef = jnp.concatenate([coef, coef], axis=1)
     ones = first_rows([jnp.ones((1, 2 * LANES), jnp.float32)] * 3, SUBLANES)
 
     def left_of(m):
@@ -141,14 +142,13 @@
     out_ref[...] = jnp.broadcast_to(block, (chips, 3 * SUBLANES, LANES))
 
 
-def contraction(coef_scale, own, other, taste):
+def contraction(own, other, taste):
     chips, markets, _, _ = taste.shape
-    smem = pl.BlockSpec(memory_space=pltpu.SMEM)
     vmem = pl.BlockSpec(memory_space=pltpu.VMEM)
     return pl.pallas_call(
         contraction_kernel,
         out_shape=jax.ShapeDtypeStruct((chips, 3 * SUBLANES, LANES), jnp.float32),
-        in_specs=[smem, vmem, vmem, vmem],
+        in_specs=[vmem, vmem, vmem],
         out_specs=vmem,
         scratch_shapes=[
             pltpu.VMEM((markets, chips, 2 * LANES, LANES), jnp.float32),
@@ -159,24 +159,40 @@
             pltpu.VMEM((3, markets, 2 * LANES), jnp.float32),
         ],
         compiler_params=pltpu.CompilerParams(vmem_limit_bytes=40 * 1024 * 1024),
-    )(coef_scale, own, other, taste)
-
-
-def take_half_kernel(core_ref, whole_ref, half_ref, sem):
+    )(own, other, taste)
+
+
+def take_half_kernel(whole_ref, half_ref, staging_ref, read_sems, write_sems):
+    pieces = read_sems.shape[0]
     count = half_ref.shape[0]
-    copy = pltpu.make_async_copy(whole_ref.at[pl.ds(core_ref[0] * count, count)], half_ref, sem)
-    copy.start()
-    copy.wait()
-
-
-def take_half(core, whole, count):
+    size = count // pieces
+    first = lax.axis_index("prod") * count
+
+    def read(i):
+        return pltpu.make_async_copy(whole_ref.at[pl.ds(first + i * size, size)], staging_ref.at[pl.ds(i * size, size)], read_sems.at[i])
+
+    def write(i):
+        return pltpu.make_async_copy(staging_ref.at[pl.ds(i * size, size)], half_ref.at[pl.ds(i * size, size)], write_sems.at[i])
+
+    for i in range(pieces):
+        read(i).start()
+    for i in range(pieces):
+        read(i).wait()
+        write(i).start()
+    for i in range(pieces):
+        write(i).wait()
+
+
+def take_half(whole, count):
+    shape = (count, *whole.shape[1:])
+    hbm = pl.BlockSpec(memory_space=pltpu.HBM)
     return pl.pallas_call(
         take_half_kernel,
-        out_shape=jax.ShapeDtypeStruct((count, *whole.shape[1:]), whole.dtype),
-        in_specs=[pl.BlockSpec(memory_space=pltpu.SMEM), pl.BlockSpec(memory_space=pltpu.HBM)],
-        out_specs=pl.BlockSpec(memory_space=pltpu.HBM),
-        scratch_shapes=[pltpu.SemaphoreType.DMA(())],
-    )(core.astype(jnp.int32).reshape(1), whole)
+        out_shape=jax.ShapeDtypeStruct(shape, whole.dtype),
+        in_specs=[hbm],
+        out_specs=hbm,
+        scratch_shapes=[pltpu.VMEM(shape, whole.dtype), pltpu.SemaphoreType.DMA((4,)), pltpu.SemaphoreType.DMA((4,))],
+    )(whole)
 
 
 def shards(start_utility, log_shares, characteristics, coef_scale, taste_draws):
@@ -186,7 +202,7 @@
     own_markets = half // chips
     core, chip = (lax.axis_index(axis).astype(jnp.uint32) for axis in ("prod", "draw"))
 
-    taste = take_half(core, taste_draws, half).reshape(chips, own_markets, coefs, LANES)
+    taste = take_half(taste_draws, half).reshape(chips, own_markets, coefs, LANES)
     taste = lax.all_to_all(taste, "draw", 0, 0, tiled=True)
 
     def packed(first):
@@ -196,10 +212,11 @@
         return jnp.concatenate([chars, utility, shares], axis=0)
 
     swap = [(0, 1), (1, 0)]
-    own = packed(core * half + chip * own_markets)
+    scale = jnp.broadcast_to(coef_scale[:, None], (coefs, LANES))
+    own = jnp.concatenate([packed(core * half + chip * own_markets), scale], axis=0)
     other = lax.ppermute(packed((1 - core) * half + chip * own_markets), "prod", swap)
 
-    blocks = contraction(coef_scale, own, other, taste)
+    blocks = contraction(own, other, taste)
     blocks = lax.all_to_all(blocks, "draw", 0, 0, tiled=True)
 
     squares = jnp.sum(blocks[:, 2 * own_markets : 2 * own_markets + 2], axis=0)

time: 73.9 us -> 58.2 us (0.79)
  Pallas kernels: 23.6 us -> 7.88 us
    pallas_call x1, Pallas kernels: 17 us -> 1.84 us  [take_half(): pl.pallas_call(take_half_kernel, out_shape=jax.ShapeDtypeStruct(shape, wh...]
  transfers between devices with their start and end apart: 4 -> 4, of which waited for: 3 -> 3; matrix products, arithmetic and copies ran while one was open for 4% -> 5% of each run, Pallas kernels for 0% -> 0%
where the time goes in v4:
time: 58.2 us; the launch traced here: 57.8 us
  starting transfers between devices  20.1 us (35%)
  waiting for transfers between devices  15 us (26%)
  blocking collectives  10.5 us (18%)
  Pallas kernels  7.88 us (14%)
  local copies, waits for them, and re-layouts  2.89 us (5%)
  other arithmetic  0.76 us (1%)
  between operations  0.7 us (1%)
    all_to_all x1, blocking collectives, shards(): blocks = lax.all_to_all(blocks, 'draw', 0, 0, tiled=True)  10.5 us
    all_to_all x1, starting transfers between devices, shards(): squares = lax.all_to_all(squares, ('mkt', 'prod'), 0, 0, tiled=True)  8.59 us
    all_to_all x1, starting transfers between devices, shards(): taste = lax.all_to_all(taste, 'draw', 0, 0, tiled=True)  7.58 us
    all_to_all x1, waiting for transfers between devices, shards(): squares = lax.all_to_all(squares, ('mkt', 'prod'), 0, 0, tiled=True)  7.31 us
    all_to_all x1, waiting for transfers between devices, shards(): taste = lax.all_to_all(taste, 'draw', 0, 0, tiled=True)  6.96 us
    pallas_call x1, Pallas kernels, contraction(): pl.pallas_call(contraction_kernel, out_shape=jax.ShapeDtypeStruct((chips,...  6.04 us
    ppermute x1, starting transfers between devices, shards(): given = lax.ppermute(given, 'prod', swap)  2.9 us
    pallas_call x1, Pallas kernels, take_half(): pl.pallas_call(take_half_kernel, out_shape=jax.ShapeDtypeStruct(shape, wh...  1.84 us
  transfers between devices with their start and end apart: 4, of which 3 were waited for; matrix products, arithmetic and copies ran while one was open for 5% of the time, Pallas kernels for 0%

profile of v4, /device:TPU:1, one launch (start us, length us, event | category | flops | bytes accessed | tf_op | source)
XLA Modules:
  0.0 57.8 jit_solution(4536783569783147982)
XLA Ops:
  0.6 1.8 %shard_map.68 = f32[128,8,128]{2,1,0:T(8,128)} custom-call(f32[256,8,128]{2,1,0:T(8,128)} %whole_ref.1), custom_call_target="tpu_custom_call" | custom-call | tf_op jit(solution)/shard_map/pallas_call | solution.py:189
  2.5 7.6 %all-to-all-start = ((f32[16,8,8,128]{3,2,1,0:T(8,128)}), f32[16,8,8,128]{3,2,1,0:T(8,128)S(1)}, u32[]{:S(2)}, u32[]{:S(2)}) async-start(f32[16,8,8,128]{3,2,1,0:T(8,128)} %bitcast.11), calls=%async_computation | async-start | bytes 1048576 | tf_op jit(solution)/shard_map/all_to_all | solution.py:206
  10.1 0.7 %constant_dynamic-slice_fusion = (f32[8,128]{1,0:T(8,128)S(1)}, f32[8,128]{1,0:T(8,128)S(1)}, f32[8,128]{1,0:T(8,128)S(1)}, f32[8,128]{1,0:T(8,128)S(1)}) fusion(f32[256,128]{1,0:T(8,128)} %param.6, u32[]{:T(128)S(6)} %add.10, u32[]{:T(128)S(6)} %add.9, f32[256,128]{1,0:T(8,128)} %param.5), kind=kLoop, calls=%fused_computation.9 | loop fusion | bytes 32776 | tf_op jit(solution)/shard_map/dynamic_slice | solution.py:211
  10.8 0.8 %dynamic-slice_bitcast_fusion = (f32[64,128]{1,0:T(8,128)S(1)}, f32[64,128]{1,0:T(8,128)S(1)}) fusion(f32[256,8,128]{2,1,0:T(8,128)} %param.7, u32[]{:T(128)S(6)} %add.10, u32[]{:T(128)S(6)} %add.9), kind=kLoop, calls=%fused_computation.5 | loop fusion | bytes 131080 | tf_op jit(solution)/shard_map/reshape | solution.py:209
  11.6 0.0 copy-start.1
  11.6 1.0 %collective-permute-start = (f32[80,128]{1,0:T(8,128)S(1)}, f32[80,128]{1,0:T(8,128)S(1)}, u32[]{:S(2)}, u32[]{:S(2)}) collective-permute-start(f32[80,128]{1,0:T(8,128)S(1)} %pad_maximum_fusion), channel_id=1, source_target_pairs={{0,16},{16,0},{1,17},{17,1},{2,18},{18,2},{3,19},{19,3},{4,20},{20... | collective-permute-start | bytes 122888 | tf_op jit(solution)/shard_map/ppermute | solution.py:217
  12.7 0.0 copy-done.1
  12.7 0.1 pad.6.clone
  12.7 0.1 maximum_maximum_fusion.own_ref
  12.8 0.7 %collective-permute-done.other_ref = f32[80,128]{1,0:T(8,128)S(1)} collective-permute-done((f32[80,128]{1,0:T(8,128)S(1)}, f32[80,128]{1,0:T(8,128)S(1)}, u32[]{:S(2)}, u32[]{:S(2)}) %collective-permute-start) | collective-permute-done | bytes 40992 | tf_op jit(solution)/shard_map/ppermute | solution.py:217
  13.5 7.0 %all-to-all-done.taste_ref = f32[16,8,8,128]{3,2,1,0:T(8,128)S(1)} async-done(((f32[16,8,8,128]{3,2,1,0:T(8,128)}), f32[16,8,8,128]{3,2,1,0:T(8,128)S(1)}, u32[]{:S(2)}, u32[]{:S(2)}) %all-to-all-start) | async-done | bytes 524320 | tf_op jit(solution)/shard_map/all_to_all | solution.py:206
  20.5 6.0 %shard_map.69 = f32[16,24,128]{2,1,0:T(8,128)S(1)} custom-call(f32[88,128]{1,0:T(8,128)S(1)} %maximum_maximum_fusion.own_ref, f32[80,128]{1,0:T(8,128)S(1)} %collective-permute-done.other_ref, f32[16,8,8,128]{3,2,1,0:T(8,128)S(1)} %all-to-all-done.taste_ref), custom_call_target="tpu_custom_call" | custom-call | tf_op jit(solution)/shard_map/pallas_call | solution.py:148
  26.5 10.5 %all_to_all.15 = f32[16,24,128]{2,1,0:T(8,128)S(1)} all-to-all(f32[16,24,128]{2,1,0:T(8,128)S(1)} %shard_map.69), channel_id=1, replica_groups=mesh['mkt'=8,'prod'=2,'draw'=16] {'draw'}, dimensions={0} | all-to-all | bytes 393216 | tf_op jit(solution)/shard_map/all_to_all | solution.py:220
  37.0 2.9 %collective-permute-start.1 = (f32[128,128]{1,0:T(8,128)S(1)}, f32[128,128]{1,0:T(8,128)S(1)}, u32[]{:S(2)}, u32[]{:S(2)}) collective-permute-start(f32[128,128]{1,0:T(8,128)S(1)} %slice_bitcast_fusion), channel_id=1, source_target_pairs={{0,16},{16,0},{1,17},{17,1},{2,18},{18,2},{3,19},{19,3},{4,20},{20... | collective-permute-start | bytes 196616 | tf_op jit(solution)/shard_map/ppermute | solution.py:227
  39.9 0.6 %broadcast_in_dim.14 = f32[16,2,128]{2,1,0:T(2,128)} broadcast(f32[2,128]{1,0:T(2,128)S(1)} %slice_reduce_fusion), dimensions={1,2} | broadcast | bytes 17408 | tf_op jit(solution)/shard_map/broadcast_in_dim | solution.py:223
  40.5 8.6 %all-to-all-start.2 = ((f32[16,2,128]{2,1,0:T(2,128)}), f32[16,2,128]{2,1,0:T(2,128)S(1)}, u32[]{:S(2)}, u32[]{:S(2)}) async-start(f32[16,2,128]{2,1,0:T(2,128)} %broadcast_in_dim.14), calls=%async_computation.2 | async-start | bytes 32768 | tf_op jit(solution)/shard_map/all_to_all | solution.py:224
  49.2 7.3 %all-to-all-done.2 = f32[16,2,128]{2,1,0:T(2,128)S(1)} async-done(((f32[16,2,128]{2,1,0:T(2,128)}), f32[16,2,128]{2,1,0:T(2,128)S(1)}, u32[]{:S(2)}, u32[]{:S(2)}) %all-to-all-start.2) | async-done | bytes 16416 | tf_op jit(solution)/shard_map/all_to_all | solution.py:224
  56.5 0.1 reduce_sum.19
  56.6 0.5 add_sqrt_fusion
  57.1 0.0 collective-permute-done.1
  57.1 0.0 copy-start
  57.2 0.6 %copy-done = f32[256,128]{1,0:T(8,128)} copy-done((f32[256,128]{1,0:T(8,128)}, f32[256,128]{1,0:T(8,128)S(1)}, u32[]{:S(2)}) %copy-start) | copy-done | bytes 131096
  (6 shorter events, 0.1 us)
Async XLA Ops:
  2.5 18.0 %all-to-all-start = ((f32[16,8,8,128]{3,2,1,0:T(8,128)}), f32[16,8,8,128]{3,2,1,0:T(8,128)S(1)}, u32[]{:S(2)}, u32[]{:S(2)}) async-start(f32[16,8,8,128]{3,2,1,0:T(8,128)} %bitcast.11), calls=%async_computation | async-start | bytes 1048576 | tf_op jit(solution)/shard_map/all_to_all | solution.py:206
  11.6 1.1 %copy-start.1 = (f32[8]{0:T(128)S(1)}, f32[8]{0:T(128)}, u32[]{:S(2)}) copy-start(f32[8]{0:T(128)} %param.8) | copy-start | bytes 100
  11.6 1.9 %collective-permute-start = (f32[80,128]{1,0:T(8,128)S(1)}, f32[80,128]{1,0:T(8,128)S(1)}, u32[]{:S(2)}, u32[]{:S(2)}) collective-permute-start(f32[80,128]{1,0:T(8,128)S(1)} %pad_maximum_fusion), channel_id=1, source_target_pairs={{0,16},{16,0},{1,17},{17,1},{2,18},{18,2},{3,19},{19,3},{4,20},{20... | collective-permute-start | bytes 122888 | tf_op jit(solution)/shard_map/ppermute | solution.py:217
  37.0 20.1 %collective-permute-start.1 = (f32[128,128]{1,0:T(8,128)S(1)}, f32[128,128]{1,0:T(8,128)S(1)}, u32[]{:S(2)}, u32[]{:S(2)}) collective-permute-start(f32[128,128]{1,0:T(8,128)S(1)} %slice_bitcast_fusion), channel_id=1, source_target_pairs={{0,16},{16,0},{1,17},{17,1},{2,18},{18,2},{3,19},{19,3},{4,20},{20... | collective-permute-start | bytes 196616 | tf_op jit(solution)/shard_map/ppermute | solution.py:227
  40.5 15.9 %all-to-all-start.2 = ((f32[16,2,128]{2,1,0:T(2,128)}), f32[16,2,128]{2,1,0:T(2,128)S(1)}, u32[]{:S(2)}, u32[]{:S(2)}) async-start(f32[16,2,128]{2,1,0:T(2,128)} %broadcast_in_dim.14), calls=%async_computation.2 | async-start | bytes 32768 | tf_op jit(solution)/shard_map/all_to_all | solution.py:224
  57.1 0.7 %copy-start = (f32[256,128]{1,0:T(8,128)}, f32[256,128]{1,0:T(8,128)S(1)}, u32[]{:S(2)}) copy-start(f32[256,128]{1,0:T(8,128)S(1)} %constant_dynamic-update-slice_fusion) | copy-start | bytes 393220

commit v5 on v3

--- a/solution.py
+++ b/solution.py
@@ -48,23 +48,27 @@
     return terms[0]
 
 
-def contraction_kernel(coef_ref, own_ref, other_ref, taste_ref, out_ref, weight_ref, inverse_ref, share_ref, factor_ref, left_ref, row_ref):
-    markets = own_ref.shape[0] // 10
-    coefs = 8
+def contraction_kernel(gate_ref, coef_ref, own_ref, other_ref, taste_ref, out_ref, weight_ref, inverse_ref, share_ref, factor_ref, left_ref, row_ref):
+    coefs = own_ref.shape[1]
+    markets = own_ref.shape[0] - 2
     chips = taste_ref.shape[0]
     groups = 2 * LANES // SUBLANES
     slices = chips // 2
 
-    def part(first, count):
-        return jnp.concatenate([own_ref[pl.ds(first, count)], other_ref[pl.ds(first, count)]], axis=1)
-
-    coef = jnp.concatenate([jnp.full((1, 2 * LANES), coef_ref[k] * LOG2E, jnp.float32) for k in range(coefs)], axis=0)
+    def part(i):
+        return jnp.concatenate([own_ref[i], other_ref[i]], axis=1)
+
+    utility, shares = part(markets), part(markets + 1)
+    square = (coefs, coefs)
+    diagonal = lax.broadcasted_iota(jnp.int32, square, 0) == lax.broadcasted_iota(jnp.int32, square, 1)
+    coef = jnp.where(diagonal, jnp.broadcast_to(coef_ref[...].reshape(1, coefs), square), 0.0)
+    coef = jnp.broadcast_to(jnp.sum(coef, axis=1, keepdims=True) * LOG2E, (coefs, 2 * LANES))
     ones = first_rows([jnp.ones((1, 2 * LANES), jnp.float32)] * 3, SUBLANES)
 
     def left_of(m):
-        chars = part(m * coefs, coefs) * coef
+        chars = part(m) * coef
         high = rounded(chars)
-        base = first_rows(three_parts(part(8 * markets + m, 1) * LOG2E), SUBLANES)
+        base = first_rows(three_parts(utility[m : m + 1] * LOG2E), SUBLANES)
         left_ref[m] = jnp.concatenate([high, high, chars - high, base], axis=0).astype(jnp.bfloat16)
 
     def weigh(m, q):
@@ -88,7 +92,7 @@
         return jnp.sum(share_ref[m].T, axis=0, keepdims=True) * (1.0 / R)
 
     def first_end(m):
-        change = part(9 * markets + m, 1) - jnp.log(predicted(m))
+        change = shares[m : m + 1] - jnp.log(predicted(m))
         factor = jnp.exp(change)
         row_ref[0, pl.ds(m, 1)] = change
         row_ref[1, pl.ds(m, 1)] = factor
@@ -130,8 +134,8 @@
             second_end(d)
 
     first_change = row_ref[0]
-    second_change = part(9 * markets, markets) - jnp.log(row_ref[1] * row_ref[2])
-    result = part(8 * markets, markets) + first_change + second_change
+    second_change = shares - jnp.log(row_ref[1] * row_ref[2])
+    result = utility + first_change + second_change
     squares = []
     for change in (first_change, second_change):
         square = change * change
@@ -141,14 +145,13 @@
     out_ref[...] = jnp.broadcast_to(block, (chips, 3 * SUBLANES, LANES))
 
 
-def contraction(coef_scale, own, other, taste):
+def contraction(gate, coef_scale, own, other, taste):
     chips, markets, _, _ = taste.shape
-    smem = pl.BlockSpec(memory_space=pltpu.SMEM)
     vmem = pl.BlockSpec(memory_space=pltpu.VMEM)
     return pl.pallas_call(
         contraction_kernel,
         out_shape=jax.ShapeDtypeStruct((chips, 3 * SUBLANES, LANES), jnp.float32),
-        in_specs=[smem, vmem, vmem, vmem],
+        in_specs=[vmem] * 5,
         out_specs=vmem,
         scratch_shapes=[
             pltpu.VMEM((markets, chips, 2 * LANES, LANES), jnp.float32),
@@ -159,24 +162,38 @@
             pltpu.VMEM((3, markets, 2 * LANES), jnp.float32),
         ],
         compiler_params=pltpu.CompilerParams(vmem_limit_bytes=40 * 1024 * 1024),
-    )(coef_scale, own, other, taste)
-
-
-def take_half_kernel(core_ref, whole_ref, half_ref, sem):
+    )(gate, coef_scale, own, other, taste)
+
+
+def pick_kernel(utility_ref, shares_ref, chars_ref, coef_ref, taste_ref, half_ref, own_ref, given_ref, scale_ref, side_ref, sems):
     count = half_ref.shape[0]
-    copy = pltpu.make_async_copy(whole_ref.at[pl.ds(core_ref[0] * count, count)], half_ref, sem)
-    copy.start()
-    copy.wait()
-
-
-def take_half(core, whole, count):
+    markets = own_ref.shape[0] - 2
+    core, chip = lax.axis_index("prod"), lax.axis_index("draw")
+    pairs = [(taste_ref.at[pl.ds(core * count, count)], half_ref), (coef_ref, scale_ref)]
+    for ref, side in ((given_ref, 1 - core), (own_ref, core)):
+        rows = pl.ds(side * count + chip * markets, markets)
+        pairs.append((chars_ref.at[rows], ref.at[pl.ds(0, markets)]))
+        pairs.append((utility_ref.at[rows], ref.at[markets]))
+        pairs.append((shares_ref.at[rows], ref.at[markets + 1]))
+    copies = [pltpu.make_async_copy(*pair, sems.at[i]) for i, pair in enumerate(pairs)]
+    for copy in copies:
+        copy.start()
+    side_ref[...] = jnp.full(side_ref.shape, core, jnp.int32)
+    for copy in copies:
+        copy.wait()
+
+
+def picked(utility, shares, chars, coef_scale, taste, count, markets):
+    hbm = pl.BlockSpec(memory_space=pltpu.HBM)
+    vmem = pl.BlockSpec(memory_space=pltpu.VMEM)
+    packed = pltpu.VMEM((markets + 2, *chars.shape[1:]), chars.dtype)
     return pl.pallas_call(
-        take_half_kernel,
-        out_shape=jax.ShapeDtypeStruct((count, *whole.shape[1:]), whole.dtype),
-        in_specs=[pl.BlockSpec(memory_space=pltpu.SMEM), pl.BlockSpec(memory_space=pltpu.HBM)],
-        out_specs=pl.BlockSpec(memory_space=pltpu.HBM),
-        scratch_shapes=[pltpu.SemaphoreType.DMA(())],
-    )(core.astype(jnp.int32).reshape(1), whole)
+        pick_kernel,
+        out_shape=[pltpu.VMEM((count, *taste.shape[1:]), taste.dtype), packed, packed, pltpu.VMEM(coef_scale.shape, coef_scale.dtype), pltpu.VMEM((1, LANES), jnp.int32)],
+        in_specs=[hbm] * 5,
+        out_specs=[vmem] * 5,
+        scratch_shapes=[pltpu.SemaphoreType.DMA((8,))],
+    )(utility, shares, chars, coef_scale, taste)
 
 
 def shards(start_utility, log_shares, characteristics, coef_scale, taste_draws):
@@ -184,33 +201,23 @@
     cores, chips, planes = lax.axis_size("prod"), lax.axis_size("draw"), lax.axis_size("mkt")
     half = markets // cores
     own_markets = half // chips
-    core, chip = (lax.axis_index(axis).astype(jnp.uint32) for axis in ("prod", "draw"))
-
-    taste = take_half(core, taste_draws, half).reshape(chips, own_markets, coefs, LANES)
-    taste = lax.all_to_all(taste, "draw", 0, 0, tiled=True)
-
-    def packed(first):
-        chars = lax.dynamic_slice_in_dim(characteristics, first, own_markets, 0).reshape(-1, LANES)
-        utility = lax.dynamic_slice_in_dim(start_utility, first, own_markets, 0)
-        shares = lax.dynamic_slice_in_dim(log_shares, first, own_markets, 0)
-        return jnp.concatenate([chars, utility, shares], axis=0)
-
     swap = [(0, 1), (1, 0)]
-    own = packed(core * half + chip * own_markets)
-    other = lax.ppermute(packed((1 - core) * half + chip * own_markets), "prod", swap)
-
-    blocks = contraction(coef_scale, own, other, taste)
+
+    taste, own, given, coef_scale, side = picked(start_utility, log_shares, characteristics, coef_scale, taste_draws, half, own_markets)
+    other = lax.ppermute(given, "prod", swap)
+    taste = lax.all_to_all(taste.reshape(chips, own_markets, coefs, LANES), "draw", 0, 0, tiled=True)
+    gate = taste[0, 0] * 0.5
+    blocks = contraction(gate, coef_scale, own, other, taste)
     blocks = lax.all_to_all(blocks, "draw", 0, 0, tiled=True)
 
     squares = jnp.sum(blocks[:, 2 * own_markets : 2 * own_markets + 2], axis=0)
     squares = jnp.broadcast_to(squares, (planes * cores, 2, LANES))
     squares = lax.all_to_all(squares, ("mkt", "prod"), 0, 0, tiled=True)
-    kept = blocks[:, :own_markets].reshape(half, LANES)
     given = blocks[:, own_markets : 2 * own_markets].reshape(half, LANES)
     given = lax.ppermute(given, "prod", swap)
-    utility = jnp.zeros((markets, LANES), jnp.float32)
-    utility = lax.dynamic_update_slice_in_dim(utility, kept, core * half, 0)
-    utility = lax.dynamic_update_slice_in_dim(utility, given, (1 - core) * half, 0)
+    kept = blocks[:, :own_markets].reshape(half, LANES)
+    first = side == 0
+    utility = jnp.concatenate([jnp.where(first, kept, given), jnp.where(first, given, kept)], axis=0)
     cells = planes * markets * cores * LANES
     return utility, jnp.sqrt(jnp.sum(squares, axis=(0, 2)) / cells + 1e-06)
 

time: 73.9 us -> 59.4 us (0.80)
  Pallas kernels: 23.6 us -> 8.71 us
  blocking collectives: 10.5 us -> 0 us
  waiting for transfers between devices: 15.1 us -> 23.7 us
  starting transfers between devices: 20.1 us -> 24 us
  local copies, waits for them, and re-layouts: 2.82 us -> 0.62 us
    pallas_call x1, Pallas kernels: 17 us -> 1.93 us  [picked(): pl.pallas_call(pick_kernel, out_shape=[pltpu.VMEM((count, *taste.shape[1:...]
    all_to_all x1 -> x0, blocking collectives: 10.5 us -> none  [shards(): blocks = lax.all_to_all(blocks, 'draw', 0, 0, tiled=True)]
    all_to_all x1 -> x2, waiting for transfers between devices: 6.97 us -> 16.5 us  [the longest x1 9.38 us: shards(): lax.all_to_all(taste.reshape(chips, own_markets, coefs, LANES), 'draw', 0...]
    all_to_all x1 -> x2, starting transfers between devices: 7.58 us -> 11.1 us  [the longest x1 7.58 us: shards(): lax.all_to_all(taste.reshape(chips, own_markets, coefs, LANES), 'draw', 0...]
    all_to_all x1, starting transfers between devices: 8.59 us -> 11.7 us  [shards(): squares = lax.all_to_all(squares, ('mkt', 'prod'), 0, 0, tiled=True)]
    ppermute x1, starting transfers between devices: 2.89 us -> 0.19 us  [shards(): given = lax.ppermute(given, 'prod', swap)]
    ppermute x1, waiting for transfers between devices: 0.86 us -> 0.01 us  [shards(): other = lax.ppermute(given, 'prod', swap)]
    reshape x1 -> x0, local copies, waits for them, and re-layouts: 0.78 us -> none  [packed(): lax.dynamic_slice_in_dim(characteristics, first, own_markets, 0)]
  transfers between devices with their start and end apart: 4 -> 5, of which waited for: 3 -> 3; matrix products, arithmetic and copies ran while one was open for 4% -> 1% of each run, Pallas kernels for 0% -> 0%
where the time goes in v5:
time: 59.4 us; the launch traced here: 59.1 us
  starting transfers between devices  24 us (40%)
  waiting for transfers between devices  23.7 us (40%)
  Pallas kernels  8.71 us (15%)
  other arithmetic  1.37 us (2%)
  between operations  0.68 us (1%)
  local copies, waits for them, and re-layouts  0.62 us (1%)
    all_to_all x1, starting transfers between devices, shards(): squares = lax.all_to_all(squares, ('mkt', 'prod'), 0, 0, tiled=True)  11.7 us
    all_to_all x1, waiting for transfers between devices, shards(): lax.all_to_all(taste.reshape(chips, own_markets, coefs, LANES), 'draw', 0...  9.38 us
    all_to_all x1, starting transfers between devices, shards(): lax.all_to_all(taste.reshape(chips, own_markets, coefs, LANES), 'draw', 0...  7.58 us
    all_to_all x1, waiting for transfers between devices, shards(): blocks = lax.all_to_all(blocks, 'draw', 0, 0, tiled=True)  7.14 us
    all_to_all x1, waiting for transfers between devices, shards(): squares = lax.all_to_all(squares, ('mkt', 'prod'), 0, 0, tiled=True)  7.13 us
    pallas_call x1, Pallas kernels, contraction(): pl.pallas_call(contraction_kernel, out_shape=jax.ShapeDtypeStruct((chips,...  6.78 us
    all_to_all x1, starting transfers between devices, shards(): blocks = lax.all_to_all(blocks, 'draw', 0, 0, tiled=True)  3.52 us
    pallas_call x1, Pallas kernels, picked(): pl.pallas_call(pick_kernel, out_shape=[pltpu.VMEM((count, *taste.shape[1:...  1.93 us
  transfers between devices with their start and end apart: 5, of which 3 were waited for; matrix products, arithmetic and copies ran while one was open for 1% of the time, Pallas kernels for 0%

profile of v5, /device:TPU:1, one launch (start us, length us, event | category | flops | bytes accessed | tf_op | source)
XLA Modules:
  0.0 59.1 jit_solution(4982634400709215380)
XLA Ops:
  0.6 1.9 %shard_map.68 = (f32[128,8,128]{2,1,0:T(8,128)}, f32[10,8,128]{2,1,0:T(8,128)S(1)}, f32[10,8,128]{2,1,0:T(8,128)S(1)}, f32[8]{0:T(128)S(1)}, s32[1,128]{1,0:T(1,128)S(1)}) custom-call(f32[256,128]{1,0:T(8,128)} %utility_ref.1, f32[256,128]{1,0:T(8,128)} %shares_ref.1, f32[256,8,128]{2,1,0:T(8,128)} %chars_ref.1, f32[8]{0:T(128)} %coef_ref.1, ...), custom_call_target="tpu_custom_call" | custom-call | tf_op jit(solution)/shard_map/pallas_call | solution.py:190
  2.6 7.6 %all-to-all-start = ((f32[16,8,8,128]{3,2,1,0:T(8,128)}), f32[16,8,8,128]{3,2,1,0:T(8,128)S(1)}, u32[]{:S(2)}, u32[]{:S(2)}) async-start(f32[16,8,8,128]{3,2,1,0:T(8,128)} %bitcast.1), calls=%async_computation | async-start | bytes 1048576 | tf_op jit(solution)/shard_map/all_to_all | solution.py:208
  10.2 1.0 %collective-permute-start = (f32[10,8,128]{2,1,0:T(8,128)S(1)}, f32[10,8,128]{2,1,0:T(8,128)S(1)}, u32[]{:S(2)}, u32[]{:S(2)}) collective-permute-start(f32[10,8,128]{2,1,0:T(8,128)S(1)} %get-tuple-element.11), channel_id=1, source_target_pairs={{0,16},{16,0},{1,17},{17,1},{2,18},{18,2},{3,19},{19,3},{4,20},{20... | collective-permute-start | bytes 122888 | tf_op jit(solution)/shard_map/ppermute | solution.py:207
  11.2 9.4 %all-to-all-done.taste_ref = f32[16,8,8,128]{3,2,1,0:T(8,128)S(1)} async-done(((f32[16,8,8,128]{3,2,1,0:T(8,128)}), f32[16,8,8,128]{3,2,1,0:T(8,128)S(1)}, u32[]{:S(2)}, u32[]{:S(2)}) %all-to-all-start) | async-done | bytes 524320 | tf_op jit(solution)/shard_map/all_to_all | solution.py:208
  20.6 0.0 collective-permute-done.other_ref
  20.6 6.8 %shard_map.69 = f32[16,24,128]{2,1,0:T(8,128)} custom-call(f32[8,128]{1,0:T(8,128)S(1)} %fusion.2.gate_ref, f32[8]{0:T(128)S(1)} %get-tuple-element.9.coef_ref, f32[10,8,128]{2,1,0:T(8,128)S(1)} %get-tuple-element.10.own_ref, f32[10,8,128]{2,1,0:T(8,128)S(1)} %collective-permute-done.other_ref, f32[16,8,8,128]{3,2,1,0:T(8,128)S(1)} %all-to-all-done.taste_ref), custom_call_target="tpu_custom_call" | custom-call | tf_op jit(solution)/shard_map/pallas_call | solution.py:151
  27.4 3.5 %all-to-all-start.1 = ((f32[16,24,128]{2,1,0:T(8,128)}), f32[16,24,128]{2,1,0:T(8,128)S(1)}, u32[]{:S(2)}, u32[]{:S(2)}) async-start(f32[16,24,128]{2,1,0:T(8,128)} %shard_map.69), calls=%async_computation.1 | async-start | bytes 393216 | tf_op jit(solution)/shard_map/all_to_all | solution.py:211
  30.9 7.1 %all-to-all-done.1 = f32[16,24,128]{2,1,0:T(8,128)S(1)} async-done(((f32[16,24,128]{2,1,0:T(8,128)}), f32[16,24,128]{2,1,0:T(8,128)S(1)}, u32[]{:S(2)}, u32[]{:S(2)}) %all-to-all-start.1) | async-done | bytes 196640 | tf_op jit(solution)/shard_map/all_to_all | solution.py:211
  38.1 0.6 %broadcast_in_dim.18 = f32[16,2,128]{2,1,0:T(2,128)} broadcast(f32[2,128]{1,0:T(2,128)S(1)} %slice_reduce_fusion), dimensions={1,2} | broadcast | bytes 17408 | tf_op jit(solution)/shard_map/broadcast_in_dim | solution.py:214
  38.7 11.7 %all-to-all-start.2 = ((f32[16,2,128]{2,1,0:T(2,128)}), f32[16,2,128]{2,1,0:T(2,128)S(1)}, u32[]{:S(2)}, u32[]{:S(2)}) async-start(f32[16,2,128]{2,1,0:T(2,128)} %broadcast_in_dim.18), calls=%async_computation.2 | async-start | bytes 32768 | tf_op jit(solution)/shard_map/all_to_all | solution.py:215
  50.4 0.2 collective-permute-start.1
  50.6 7.1 %all-to-all-done.2 = f32[16,2,128]{2,1,0:T(2,128)S(1)} async-done(((f32[16,2,128]{2,1,0:T(2,128)}), f32[16,2,128]{2,1,0:T(2,128)S(1)}, u32[]{:S(2)}, u32[]{:S(2)}) %all-to-all-start.2) | async-done | bytes 16416 | tf_op jit(solution)/shard_map/all_to_all | solution.py:215
  57.7 0.1 reduce_sum.19
  57.9 0.5 add_sqrt_fusion
  58.4 0.0 collective-permute-done.1
  58.4 0.7 %pad_maximum_fusion = f32[256,128]{1,0:T(8,128)} fusion(f32[128,128]{1,0:T(8,128)S(1)} %get-tuple-element.13, f32[128,128]{1,0:T(8,128)S(1)} %get-tuple-element.12), kind=kLoop, calls=%fused_computation | loop fusion | flops 32768 | bytes 262144 | tf_op jit(solution)/shard_map/concatenate | solution.py:220
  (5 shorter events, 0.0 us)
Async XLA Ops:
  2.6 18.0 %all-to-all-start = ((f32[16,8,8,128]{3,2,1,0:T(8,128)}), f32[16,8,8,128]{3,2,1,0:T(8,128)S(1)}, u32[]{:S(2)}, u32[]{:S(2)}) async-start(f32[16,8,8,128]{3,2,1,0:T(8,128)} %bitcast.1), calls=%async_computation | async-start | bytes 1048576 | tf_op jit(solution)/shard_map/all_to_all | solution.py:208
  10.2 10.4 %collective-permute-start = (f32[10,8,128]{2,1,0:T(8,128)S(1)}, f32[10,8,128]{2,1,0:T(8,128)S(1)}, u32[]{:S(2)}, u32[]{:S(2)}) collective-permute-start(f32[10,8,128]{2,1,0:T(8,128)S(1)} %get-tuple-element.11), channel_id=1, source_target_pairs={{0,16},{16,0},{1,17},{17,1},{2,18},{18,2},{3,19},{19,3},{4,20},{20... | collective-permute-start | bytes 122888 | tf_op jit(solution)/shard_map/ppermute | solution.py:207
  27.4 10.7 %all-to-all-start.1 = ((f32[16,24,128]{2,1,0:T(8,128)}), f32[16,24,128]{2,1,0:T(8,128)S(1)}, u32[]{:S(2)}, u32[]{:S(2)}) async-start(f32[16,24,128]{2,1,0:T(8,128)} %shard_map.69), calls=%async_computation.1 | async-start | bytes 393216 | tf_op jit(solution)/shard_map/all_to_all | solution.py:211
  38.7 19.0 %all-to-all-start.2 = ((f32[16,2,128]{2,1,0:T(2,128)}), f32[16,2,128]{2,1,0:T(2,128)S(1)}, u32[]{:S(2)}, u32[]{:S(2)}) async-start(f32[16,2,128]{2,1,0:T(2,128)} %broadcast_in_dim.18), calls=%async_computation.2 | async-start | bytes 32768 | tf_op jit(solution)/shard_map/all_to_all | solution.py:215
  50.4 8.0 %collective-permute-start.1 = (f32[128,128]{1,0:T(8,128)S(1)}, f32[128,128]{1,0:T(8,128)S(1)}, u32[]{:S(2)}, u32[]{:S(2)}) collective-permute-start(f32[128,128]{1,0:T(8,128)S(1)} %slice_bitcast_fusion), channel_id=1, source_target_pairs={{0,16},{16,0},{1,17},{17,1},{2,18},{18,2},{3,19},{19,3},{4,20},{20... | collective-permute-start | bytes 196616 | tf_op jit(solution)/shard_map/ppermute | solution.py:217

commit v6 on v3

--- a/solution.py
+++ b/solution.py
@@ -48,9 +48,9 @@
     return terms[0]
 
 
-def contraction_kernel(coef_ref, own_ref, other_ref, taste_ref, out_ref, weight_ref, inverse_ref, share_ref, factor_ref, left_ref, row_ref):
-    markets = own_ref.shape[0] // 10
+def contraction_kernel(draws_ref, own_ref, other_ref, taste_ref, out_ref, weight_ref, inverse_ref, share_ref, factor_ref, left_ref, row_ref):
     coefs = 8
+    markets = other_ref.shape[0] // (coefs + 2)
     chips = taste_ref.shape[0]
     groups = 2 * LANES // SUBLANES
     slices = chips // 2
@@ -58,7 +58,8 @@
     def part(first, count):
         return jnp.concatenate([own_ref[pl.ds(first, count)], other_ref[pl.ds(first, count)]], axis=1)
 
-    coef = jnp.concatenate([jnp.full((1, 2 * LANES), coef_ref[k] * LOG2E, jnp.float32) for k in range(coefs)], axis=0)
+    coef = own_ref[pl.ds((coefs + 2) * markets, coefs)] * LOG2E
+    coef = jnp.concatenate([coef, coef], axis=1)
     ones = first_rows([jnp.ones((1, 2 * LANES), jnp.float32)] * 3, SUBLANES)
 
     def left_of(m):
@@ -141,14 +142,13 @@
     out_ref[...] = jnp.broadcast_to(block, (chips, 3 * SUBLANES, LANES))
 
 
-def contraction(coef_scale, own, other, taste):
+def contraction(draws, own, other, taste):
     chips, markets, _, _ = taste.shape
-    smem = pl.BlockSpec(memory_space=pltpu.SMEM)
     vmem = pl.BlockSpec(memory_space=pltpu.VMEM)
     return pl.pallas_call(
         contraction_kernel,
         out_shape=jax.ShapeDtypeStruct((chips, 3 * SUBLANES, LANES), jnp.float32),
-        in_specs=[smem, vmem, vmem, vmem],
+        in_specs=[pl.BlockSpec(memory_space=pltpu.HBM), vmem, vmem, vmem],
         out_specs=vmem,
         scratch_shapes=[
             pltpu.VMEM((markets, chips, 2 * LANES, LANES), jnp.float32),
@@ -159,24 +159,7 @@
             pltpu.VMEM((3, markets, 2 * LANES), jnp.float32),
         ],
         compiler_params=pltpu.CompilerParams(vmem_limit_bytes=40 * 1024 * 1024),
-    )(coef_scale, own, other, taste)
-
-
-def take_half_kernel(core_ref, whole_ref, half_ref, sem):
-    count = half_ref.shape[0]
-    copy = pltpu.make_async_copy(whole_ref.at[pl.ds(core_ref[0] * count, count)], half_ref, sem)
-    copy.start()
-    copy.wait()
-
-
-def take_half(core, whole, count):
-    return pl.pallas_call(
-        take_half_kernel,
-        out_shape=jax.ShapeDtypeStruct((count, *whole.shape[1:]), whole.dtype),
-        in_specs=[pl.BlockSpec(memory_space=pltpu.SMEM), pl.BlockSpec(memory_space=pltpu.HBM)],
-        out_specs=pl.BlockSpec(memory_space=pltpu.HBM),
-        scratch_shapes=[pltpu.SemaphoreType.DMA(())],
-    )(core.astype(jnp.int32).reshape(1), whole)
+    )(draws, own, other, taste)
 
 
 def shards(start_utility, log_shares, characteristics, coef_scale, taste_draws):
@@ -186,7 +169,7 @@
     own_markets = half // chips
     core, chip = (lax.axis_index(axis).astype(jnp.uint32) for axis in ("prod", "draw"))
 
-    taste = take_half(core, taste_draws, half).reshape(chips, own_markets, coefs, LANES)
+    taste = lax.dynamic_slice_in_dim(taste_draws, core * half, half, 0).reshape(chips, own_markets, coefs, LANES)
     taste = lax.all_to_all(taste, "draw", 0, 0, tiled=True)
 
     def packed(first):
@@ -196,10 +179,11 @@
         return jnp.concatenate([chars, utility, shares], axis=0)
 
     swap = [(0, 1), (1, 0)]
-    own = packed(core * half + chip * own_markets)
+    scale = jnp.broadcast_to(coef_scale[:, None], (coefs, LANES))
+    own = jnp.concatenate([packed(core * half + chip * own_markets), scale], axis=0)
     other = lax.ppermute(packed((1 - core) * half + chip * own_markets), "prod", swap)
 
-    blocks = contraction(coef_scale, own, other, taste)
+    blocks = contraction(taste_draws, own, other, taste)
     blocks = lax.all_to_all(blocks, "draw", 0, 0, tiled=True)
 
     squares = jnp.sum(blocks[:, 2 * own_markets : 2 * own_markets + 2], axis=0)

time: 73.9 us -> 58.3 us (0.79)
  Pallas kernels: 23.6 us -> 6.05 us
  local copies, waits for them, and re-layouts: 2.82 us -> 4.85 us
    pallas_call x1 -> x0, Pallas kernels: 17 us -> none  [take_half(): pl.pallas_call(take_half_kernel, out_shape=jax.ShapeDtypeStruct((count, *...]
    dynamic_slice x0 -> x1, local copies, waits for them, and re-layouts: none -> 1.95 us  [shards(): lax.dynamic_slice_in_dim(taste_draws, core * half, half, 0)]
  transfers between devices with their start and end apart: 4 -> 4, of which waited for: 3 -> 3; matrix products, arithmetic and copies ran while one was open for 4% -> 5% of each run, Pallas kernels for 0% -> 0%
where the time goes in v6:
time: 58.3 us; the launch traced here: 57.9 us
  starting transfers between devices  20.1 us (34%)
  waiting for transfers between devices  15 us (26%)
  blocking collectives  10.5 us (18%)
  Pallas kernels  6.05 us (10%)
  local copies, waits for them, and re-layouts  4.85 us (8%)
  other arithmetic  0.76 us (1%)
  between operations  0.71 us (1%)
    all_to_all x1, blocking collectives, shards(): blocks = lax.all_to_all(blocks, 'draw', 0, 0, tiled=True)  10.5 us
    all_to_all x1, starting transfers between devices, shards(): squares = lax.all_to_all(squares, ('mkt', 'prod'), 0, 0, tiled=True)  8.59 us
    all_to_all x1, starting transfers between devices, shards(): taste = lax.all_to_all(taste, 'draw', 0, 0, tiled=True)  7.57 us
    all_to_all x1, waiting for transfers between devices, shards(): squares = lax.all_to_all(squares, ('mkt', 'prod'), 0, 0, tiled=True)  7.31 us
    all_to_all x1, waiting for transfers between devices, shards(): taste = lax.all_to_all(taste, 'draw', 0, 0, tiled=True)  6.96 us
    pallas_call x1, Pallas kernels, contraction(): pl.pallas_call(contraction_kernel, out_shape=jax.ShapeDtypeStruct((chips,...  6.05 us
    ppermute x1, starting transfers between devices, shards(): given = lax.ppermute(given, 'prod', swap)  2.88 us
    dynamic_slice x1, local copies, waits for them, and re-layouts, shards(): lax.dynamic_slice_in_dim(taste_draws, core * half, half, 0)  1.95 us
  transfers between devices with their start and end apart: 4, of which 3 were waited for; matrix products, arithmetic and copies ran while one was open for 5% of the time, Pallas kernels for 0%

profile of v6, /device:TPU:1, one launch (start us, length us, event | category | flops | bytes accessed | tf_op | source)
XLA Modules:
  0.0 57.9 jit_solution(2715338306004298805)
XLA Ops:
  0.6 0.0 copy-start
  0.6 2.0 %constant_dynamic-slice_fusion = f32[128,8,128]{2,1,0:T(8,128)} fusion(f32[256,8,128]{2,1,0:T(8,128)} %draws_ref.1, u32[]{:T(128)S(6)} %mul.6), kind=kLoop, calls=%fused_computation.9 | loop fusion | bytes 1048580 | tf_op jit(solution)/shard_map/dynamic_slice | solution.py:172
  2.6 7.6 %all-to-all-start = ((f32[16,8,8,128]{3,2,1,0:T(8,128)}), f32[16,8,8,128]{3,2,1,0:T(8,128)S(1)}, u32[]{:S(2)}, u32[]{:S(2)}) async-start(f32[16,8,8,128]{3,2,1,0:T(8,128)} %bitcast.2), calls=%async_computation | async-start | bytes 1048576 | tf_op jit(solution)/shard_map/all_to_all | solution.py:173
  10.2 0.7 %constant_dynamic-slice_fusion.1 = (f32[8,128]{1,0:T(8,128)S(1)}, f32[8,128]{1,0:T(8,128)S(1)}, f32[8,128]{1,0:T(8,128)S(1)}, f32[8,128]{1,0:T(8,128)S(1)}) fusion(f32[256,128]{1,0:T(8,128)} %param.6, u32[]{:T(128)S(6)} %add.10, u32[]{:T(128)S(6)} %add.9, f32[256,128]{1,0:T(8,128)} %param.5), kind=kLoop, calls=%fused_computation.10 | loop fusion | bytes 32776 | tf_op jit(solution)/shard_map/dynamic_slice | solution.py:178
  10.9 0.8 %dynamic-slice_bitcast_fusion = (f32[64,128]{1,0:T(8,128)S(1)}, f32[64,128]{1,0:T(8,128)S(1)}) fusion(f32[256,8,128]{2,1,0:T(8,128)} %param.7, u32[]{:T(128)S(6)} %add.10, u32[]{:T(128)S(6)} %add.9), kind=kLoop, calls=%fused_computation.5 | loop fusion | bytes 131080 | tf_op jit(solution)/shard_map/reshape | solution.py:176
  11.7 0.0 copy-start.2
  11.7 1.0 %collective-permute-start = (f32[80,128]{1,0:T(8,128)S(1)}, f32[80,128]{1,0:T(8,128)S(1)}, u32[]{:S(2)}, u32[]{:S(2)}) collective-permute-start(f32[80,128]{1,0:T(8,128)S(1)} %pad_maximum_fusion), channel_id=1, source_target_pairs={{0,16},{16,0},{1,17},{17,1},{2,18},{18,2},{3,19},{19,3},{4,20},{20... | collective-permute-start | bytes 122888 | tf_op jit(solution)/shard_map/ppermute | solution.py:184
  12.8 0.0 copy-done.2
  12.8 0.1 pad.6.clone
  12.8 0.1 maximum_maximum_fusion.own_ref
  12.9 0.7 %collective-permute-done.other_ref = f32[80,128]{1,0:T(8,128)S(1)} collective-permute-done((f32[80,128]{1,0:T(8,128)S(1)}, f32[80,128]{1,0:T(8,128)S(1)}, u32[]{:S(2)}, u32[]{:S(2)}) %collective-permute-start) | collective-permute-done | bytes 40992 | tf_op jit(solution)/shard_map/ppermute | solution.py:184
  13.6 7.0 %all-to-all-done.taste_ref = f32[16,8,8,128]{3,2,1,0:T(8,128)S(1)} async-done(((f32[16,8,8,128]{3,2,1,0:T(8,128)}), f32[16,8,8,128]{3,2,1,0:T(8,128)S(1)}, u32[]{:S(2)}, u32[]{:S(2)}) %all-to-all-start) | async-done | bytes 524320 | tf_op jit(solution)/shard_map/all_to_all | solution.py:173
  20.6 0.0 copy-done
  20.6 6.0 %shard_map.68 = f32[16,24,128]{2,1,0:T(8,128)S(1)} custom-call(f32[256,8,128]{2,1,0:T(8,128)S(1)} %copy-done, f32[88,128]{1,0:T(8,128)S(1)} %maximum_maximum_fusion.own_ref, f32[80,128]{1,0:T(8,128)S(1)} %collective-permute-done.other_ref, f32[16,8,8,128]{3,2,1,0:T(8,128)S(1)} %all-to-all-done.taste_ref), custom_call_target="tpu_custom_call" | custom-call | tf_op jit(solution)/shard_map/pallas_call | solution.py:148
  26.7 10.5 %all_to_all.15 = f32[16,24,128]{2,1,0:T(8,128)S(1)} all-to-all(f32[16,24,128]{2,1,0:T(8,128)S(1)} %shard_map.68), channel_id=1, replica_groups=mesh['mkt'=8,'prod'=2,'draw'=16] {'draw'}, dimensions={0} | all-to-all | bytes 393216 | tf_op jit(solution)/shard_map/all_to_all | solution.py:187
  37.1 2.9 %collective-permute-start.1 = (f32[128,128]{1,0:T(8,128)S(1)}, f32[128,128]{1,0:T(8,128)S(1)}, u32[]{:S(2)}, u32[]{:S(2)}) collective-permute-start(f32[128,128]{1,0:T(8,128)S(1)} %slice_bitcast_fusion), channel_id=1, source_target_pairs={{0,16},{16,0},{1,17},{17,1},{2,18},{18,2},{3,19},{19,3},{4,20},{20... | collective-permute-start | bytes 196616 | tf_op jit(solution)/shard_map/ppermute | solution.py:194
  40.0 0.6 %broadcast_in_dim.14 = f32[16,2,128]{2,1,0:T(2,128)} broadcast(f32[2,128]{1,0:T(2,128)S(1)} %slice_reduce_fusion), dimensions={1,2} | broadcast | bytes 17408 | tf_op jit(solution)/shard_map/broadcast_in_dim | solution.py:190
  40.7 8.6 %all-to-all-start.2 = ((f32[16,2,128]{2,1,0:T(2,128)}), f32[16,2,128]{2,1,0:T(2,128)S(1)}, u32[]{:S(2)}, u32[]{:S(2)}) async-start(f32[16,2,128]{2,1,0:T(2,128)} %broadcast_in_dim.14), calls=%async_computation.2 | async-start | bytes 32768 | tf_op jit(solution)/shard_map/all_to_all | solution.py:191
  49.3 7.3 %all-to-all-done.2 = f32[16,2,128]{2,1,0:T(2,128)S(1)} async-done(((f32[16,2,128]{2,1,0:T(2,128)}), f32[16,2,128]{2,1,0:T(2,128)S(1)}, u32[]{:S(2)}, u32[]{:S(2)}) %all-to-all-start.2) | async-done | bytes 16416 | tf_op jit(solution)/shard_map/all_to_all | solution.py:191
  56.6 0.1 reduce_sum.19
  56.7 0.5 add_sqrt_fusion
  57.2 0.0 collective-permute-done.1
  57.3 0.0 copy-start.1
  57.3 0.6 %copy-done.1 = f32[256,128]{1,0:T(8,128)} copy-done((f32[256,128]{1,0:T(8,128)}, f32[256,128]{1,0:T(8,128)S(1)}, u32[]{:S(2)}) %copy-start.1) | copy-done | bytes 131096
  (6 shorter events, 0.1 us)
Async XLA Ops:
  0.6 20.0 %copy-start = (f32[256,8,128]{2,1,0:T(8,128)S(1)}, f32[256,8,128]{2,1,0:T(8,128)}, u32[]{:S(2)}) copy-start(f32[256,8,128]{2,1,0:T(8,128)} %draws_ref.1) | copy-start | bytes 3145732
  2.6 18.0 %all-to-all-start = ((f32[16,8,8,128]{3,2,1,0:T(8,128)}), f32[16,8,8,128]{3,2,1,0:T(8,128)S(1)}, u32[]{:S(2)}, u32[]{:S(2)}) async-start(f32[16,8,8,128]{3,2,1,0:T(8,128)} %bitcast.2), calls=%async_computation | async-start | bytes 1048576 | tf_op jit(solution)/shard_map/all_to_all | solution.py:173
  11.7 1.1 %copy-start.2 = (f32[8]{0:T(128)S(1)}, f32[8]{0:T(128)}, u32[]{:S(2)}) copy-start(f32[8]{0:T(128)} %param.8) | copy-start | bytes 100
  11.7 1.9 %collective-permute-start = (f32[80,128]{1,0:T(8,128)S(1)}, f32[80,128]{1,0:T(8,128)S(1)}, u32[]{:S(2)}, u32[]{:S(2)}) collective-permute-start(f32[80,128]{1,0:T(8,128)S(1)} %pad_maximum_fusion), channel_id=1, source_target_pairs={{0,16},{16,0},{1,17},{17,1},{2,18},{18,2},{3,19},{19,3},{4,20},{20... | collective-permute-start | bytes 122888 | tf_op jit(solution)/shard_map/ppermute | solution.py:184
  37.1 20.1 %collective-permute-start.1 = (f32[128,128]{1,0:T(8,128)S(1)}, f32[128,128]{1,0:T(8,128)S(1)}, u32[]{:S(2)}, u32[]{:S(2)}) collective-permute-start(f32[128,128]{1,0:T(8,128)S(1)} %slice_bitcast_fusion), channel_id=1, source_target_pairs={{0,16},{16,0},{1,17},{17,1},{2,18},{18,2},{3,19},{19,3},{4,20},{20... | collective-permute-start | bytes 196616 | tf_op jit(solution)/shard_map/ppermute | solution.py:194
  40.7 15.9 %all-to-all-start.2 = ((f32[16,2,128]{2,1,0:T(2,128)}), f32[16,2,128]{2,1,0:T(2,128)S(1)}, u32[]{:S(2)}, u32[]{:S(2)}) async-start(f32[16,2,128]{2,1,0:T(2,128)} %broadcast_in_dim.14), calls=%async_computation.2 | async-start | bytes 32768 | tf_op jit(solution)/shard_map/all_to_all | solution.py:191
  57.3 0.7 %copy-start.1 = (f32[256,128]{1,0:T(8,128)}, f32[256,128]{1,0:T(8,128)S(1)}, u32[]{:S(2)}) copy-start(f32[256,128]{1,0:T(8,128)S(1)} %constant_dynamic-update-slice_fusion) | copy-start | bytes 393220

commit v7 on v4

--- a/solution.py
+++ b/solution.py
@@ -11,6 +11,14 @@
 LOG2E = math.log2(math.e)
 LANES = 128
 SUBLANES = 8
+
+
+FIRST_CHIP = 10
+FIRST_PLACE = 8
+
+
+def led_by(first, count):
+    return [[(first + i) % count for i in range(count)]]
 
 
 def rounded(x):
@@ -201,9 +209,11 @@
     half = markets // cores
     own_markets = half // chips
     core, chip = (lax.axis_index(axis).astype(jnp.uint32) for axis in ("prod", "draw"))
+    plane, meeting = led_by(FIRST_CHIP, chips), led_by(FIRST_PLACE, planes * cores)
+    chip = (chip + chips - FIRST_CHIP) % chips
 
     taste = take_half(taste_draws, half).reshape(chips, own_markets, coefs, LANES)
-    taste = lax.all_to_all(taste, "draw", 0, 0, tiled=True)
+    taste = lax.all_to_all(taste, "draw", 0, 0, axis_index_groups=plane, tiled=True)
 
     def packed(first):
         chars = lax.dynamic_slice_in_dim(characteristics, first, own_markets, 0).reshape(-1, LANES)
@@ -217,11 +227,11 @@
     other = lax.ppermute(packed((1 - core) * half + chip * own_markets), "prod", swap)
 
     blocks = contraction(own, other, taste)
-    blocks = lax.all_to_all(blocks, "draw", 0, 0, tiled=True)
+    blocks = lax.all_to_all(blocks, "draw", 0, 0, axis_index_groups=plane, tiled=True)
 
     squares = jnp.sum(blocks[:, 2 * own_markets : 2 * own_markets + 2], axis=0)
     squares = jnp.broadcast_to(squares, (planes * cores, 2, LANES))
-    squares = lax.all_to_all(squares, ("mkt", "prod"), 0, 0, tiled=True)
+    squares = lax.all_to_all(squares, ("mkt", "prod"), 0, 0, axis_index_groups=meeting, tiled=True)
     kept = blocks[:, :own_markets].reshape(half, LANES)
     given = blocks[:, own_markets : 2 * own_markets].reshape(half, LANES)
     given = lax.ppermute(given, "prod", swap)

time: 58.2 us -> 51.5 us (0.88)
  waiting for transfers between devices: 15 us -> 6.59 us
  starting transfers between devices: 20.1 us -> 23 us
  blocking collectives: 10.5 us -> 9.26 us
    all_to_all x2, waiting for transfers between devices: 14.3 us -> 5.88 us  [the longest x1 3.47 us: shards(): lax.all_to_all(taste, 'draw', 0, 0, axis_index_groups=plane, tiled=True)]
    all_to_all x2, starting transfers between devices: 16.2 us -> 19.7 us  [the longest x1 10.1 us: shards(): lax.all_to_all(squares, ('mkt', 'prod'), 0, 0, axis_index_groups=meeting,...]
    all_to_all x1, blocking collectives: 10.5 us -> 9.26 us  [shards(): lax.all_to_all(blocks, 'draw', 0, 0, axis_index_groups=plane, tiled=True)]
    ppermute x1, starting transfers between devices: 2.9 us -> 2.25 us  [shards(): given = lax.ppermute(given, 'prod', swap)]
  transfers between devices with their start and end apart: 4 -> 4, of which waited for: 3 -> 3; matrix products, arithmetic and copies ran while one was open for 5% -> 6% of each run, Pallas kernels for 0% -> 0%
where the time goes in v7:
time: 51.5 us; the launch traced here: 51.1 us
  starting transfers between devices  23 us (45%)
  blocking collectives  9.26 us (18%)
  Pallas kernels  7.89 us (15%)
  waiting for transfers between devices  6.59 us (13%)
  local copies, waits for them, and re-layouts  2.89 us (6%)
  other arithmetic  0.76 us (1%)
  between operations  0.68 us (1%)
    all_to_all x1, starting transfers between devices, shards(): lax.all_to_all(squares, ('mkt', 'prod'), 0, 0, axis_index_groups=meeting,...  10.1 us
    all_to_all x1, starting transfers between devices, shards(): lax.all_to_all(taste, 'draw', 0, 0, axis_index_groups=plane, tiled=True)  9.6 us
    all_to_all x1, blocking collectives, shards(): lax.all_to_all(blocks, 'draw', 0, 0, axis_index_groups=plane, tiled=True)  9.26 us
    pallas_call x1, Pallas kernels, contraction(): pl.pallas_call(contraction_kernel, out_shape=jax.ShapeDtypeStruct((chips,...  6.05 us
    all_to_all x1, waiting for transfers between devices, shards(): lax.all_to_all(taste, 'draw', 0, 0, axis_index_groups=plane, tiled=True)  3.47 us
    all_to_all x1, waiting for transfers between devices, shards(): lax.all_to_all(squares, ('mkt', 'prod'), 0, 0, axis_index_groups=meeting,...  2.41 us
    ppermute x1, starting transfers between devices, shards(): given = lax.ppermute(given, 'prod', swap)  2.25 us
    pallas_call x1, Pallas kernels, take_half(): pl.pallas_call(take_half_kernel, out_shape=jax.ShapeDtypeStruct(shape, wh...  1.84 us
  transfers between devices with their start and end apart: 4, of which 3 were waited for; matrix products, arithmetic and copies ran while one was open for 6% of the time, Pallas kernels for 0%

profile of v7, /device:TPU:1, one launch (start us, length us, event | category | flops | bytes accessed | tf_op | source)
XLA Modules:
  0.0 51.1 jit_solution(9123314046905183705)
XLA Ops:
  0.6 1.8 %shard_map.68 = f32[128,8,128]{2,1,0:T(8,128)} custom-call(f32[256,8,128]{2,1,0:T(8,128)} %whole_ref.1), custom_call_target="tpu_custom_call" | custom-call | tf_op jit(solution)/shard_map/pallas_call | solution.py:197
  2.5 9.6 %all-to-all-start = ((f32[16,8,8,128]{3,2,1,0:T(8,128)}), f32[16,8,8,128]{3,2,1,0:T(8,128)S(1)}, u32[]{:S(2)}, u32[]{:S(2)}) async-start(f32[16,8,8,128]{3,2,1,0:T(8,128)} %bitcast.11), calls=%async_computation | async-start | bytes 1048576 | tf_op jit(solution)/shard_map/all_to_all | solution.py:216
  12.1 0.7 %constant_dynamic-slice_fusion = (f32[8,128]{1,0:T(8,128)S(1)}, f32[8,128]{1,0:T(8,128)S(1)}, f32[8,128]{1,0:T(8,128)S(1)}, f32[8,128]{1,0:T(8,128)S(1)}) fusion(f32[256,128]{1,0:T(8,128)} %param.6, u32[]{:T(128)S(6)} %add.16, u32[]{:T(128)S(6)} %add.15, f32[256,128]{1,0:T(8,128)} %param.5), kind=kLoop, calls=%fused_computation.9 | loop fusion | bytes 32776 | tf_op jit(solution)/shard_map/dynamic_slice | solution.py:221
  12.8 0.8 %dynamic-slice_bitcast_fusion = (f32[64,128]{1,0:T(8,128)S(1)}, f32[64,128]{1,0:T(8,128)S(1)}) fusion(f32[256,8,128]{2,1,0:T(8,128)} %param.7, u32[]{:T(128)S(6)} %add.16, u32[]{:T(128)S(6)} %add.15), kind=kLoop, calls=%fused_computation.5 | loop fusion | bytes 131080 | tf_op jit(solution)/shard_map/reshape | solution.py:219
  13.6 0.0 copy-start.1
  13.6 1.0 %collective-permute-start = (f32[80,128]{1,0:T(8,128)S(1)}, f32[80,128]{1,0:T(8,128)S(1)}, u32[]{:S(2)}, u32[]{:S(2)}) collective-permute-start(f32[80,128]{1,0:T(8,128)S(1)} %pad_maximum_fusion), channel_id=1, source_target_pairs={{0,16},{16,0},{1,17},{17,1},{2,18},{18,2},{3,19},{19,3},{4,20},{20... | collective-permute-start | bytes 122888 | tf_op jit(solution)/shard_map/ppermute | solution.py:227
  14.6 0.0 copy-done.1
  14.6 0.1 pad.6.clone
  14.7 0.1 maximum_maximum_fusion.own_ref
  14.8 0.7 %collective-permute-done.other_ref = f32[80,128]{1,0:T(8,128)S(1)} collective-permute-done((f32[80,128]{1,0:T(8,128)S(1)}, f32[80,128]{1,0:T(8,128)S(1)}, u32[]{:S(2)}, u32[]{:S(2)}) %collective-permute-start) | collective-permute-done | bytes 40992 | tf_op jit(solution)/shard_map/ppermute | solution.py:227
  15.5 3.5 %all-to-all-done.taste_ref = f32[16,8,8,128]{3,2,1,0:T(8,128)S(1)} async-done(((f32[16,8,8,128]{3,2,1,0:T(8,128)}), f32[16,8,8,128]{3,2,1,0:T(8,128)S(1)}, u32[]{:S(2)}, u32[]{:S(2)}) %all-to-all-start) | async-done | bytes 524320 | tf_op jit(solution)/shard_map/all_to_all | solution.py:216
  19.0 6.1 %shard_map.69 = f32[16,24,128]{2,1,0:T(8,128)S(1)} custom-call(f32[88,128]{1,0:T(8,128)S(1)} %maximum_maximum_fusion.own_ref, f32[80,128]{1,0:T(8,128)S(1)} %collective-permute-done.other_ref, f32[16,8,8,128]{3,2,1,0:T(8,128)S(1)} %all-to-all-done.taste_ref), custom_call_target="tpu_custom_call" | custom-call | tf_op jit(solution)/shard_map/pallas_call | solution.py:156
  25.0 9.3 %all_to_all.15 = f32[16,24,128]{2,1,0:T(8,128)S(1)} all-to-all(f32[16,24,128]{2,1,0:T(8,128)S(1)} %shard_map.69), channel_id=1, replica_groups={{10,11,12,13,14,15,0,1,2,3,4,5,6,7,8,9},{26,27,28,29,30,31,16,17,18,19,..., dimensions={0} | all-to-all | bytes 393216 | tf_op jit(solution)/shard_map/all_to_all | solution.py:230
  34.3 2.2 %collective-permute-start.1 = (f32[128,128]{1,0:T(8,128)S(1)}, f32[128,128]{1,0:T(8,128)S(1)}, u32[]{:S(2)}, u32[]{:S(2)}) collective-permute-start(f32[128,128]{1,0:T(8,128)S(1)} %slice_bitcast_fusion), channel_id=1, source_target_pairs={{0,16},{16,0},{1,17},{17,1},{2,18},{18,2},{3,19},{19,3},{4,20},{20... | collective-permute-start | bytes 196616 | tf_op jit(solution)/shard_map/ppermute | solution.py:237
  36.6 0.6 %broadcast_in_dim.14 = f32[16,2,128]{2,1,0:T(2,128)} broadcast(f32[2,128]{1,0:T(2,128)S(1)} %slice_reduce_fusion), dimensions={1,2} | broadcast | bytes 17408 | tf_op jit(solution)/shard_map/broadcast_in_dim | solution.py:233
  37.2 10.1 %all-to-all-start.2 = ((f32[16,2,128]{2,1,0:T(2,128)}), f32[16,2,128]{2,1,0:T(2,128)S(1)}, u32[]{:S(2)}, u32[]{:S(2)}) async-start(f32[16,2,128]{2,1,0:T(2,128)} %broadcast_in_dim.14), calls=%async_computation.2 | async-start | bytes 32768 | tf_op jit(solution)/shard_map/all_to_all | solution.py:234
  47.4 2.4 %all-to-all-done.2 = f32[16,2,128]{2,1,0:T(2,128)S(1)} async-done(((f32[16,2,128]{2,1,0:T(2,128)}), f32[16,2,128]{2,1,0:T(2,128)S(1)}, u32[]{:S(2)}, u32[]{:S(2)}) %all-to-all-start.2) | async-done | bytes 16416 | tf_op jit(solution)/shard_map/all_to_all | solution.py:234
  49.8 0.1 reduce_sum.19
  49.9 0.5 %add_sqrt_fusion = f32[2]{0:T(128)} fusion(f32[2]{0:T(128)S(1)} %reduce_sum.19), kind=kLoop, calls=%fused_computation.13 | loop fusion | flops 4 | bytes 16 | tf_op jit(solution)/shard_map/sqrt | solution.py:242
  50.4 0.0 collective-permute-done.1
  50.4 0.0 copy-start
  50.5 0.6 %copy-done = f32[256,128]{1,0:T(8,128)} copy-done((f32[256,128]{1,0:T(8,128)}, f32[256,128]{1,0:T(8,128)S(1)}, u32[]{:S(2)}) %copy-start) | copy-done | bytes 131096
  (6 shorter events, 0.1 us)
Async XLA Ops:
  2.5 16.5 %all-to-all-start = ((f32[16,8,8,128]{3,2,1,0:T(8,128)}), f32[16,8,8,128]{3,2,1,0:T(8,128)S(1)}, u32[]{:S(2)}, u32[]{:S(2)}) async-start(f32[16,8,8,128]{3,2,1,0:T(8,128)} %bitcast.11), calls=%async_computation | async-start | bytes 1048576 | tf_op jit(solution)/shard_map/all_to_all | solution.py:216
  13.6 1.1 %copy-start.1 = (f32[8]{0:T(128)S(1)}, f32[8]{0:T(128)}, u32[]{:S(2)}) copy-start(f32[8]{0:T(128)} %param.8) | copy-start | bytes 100
  13.6 1.9 %collective-permute-start = (f32[80,128]{1,0:T(8,128)S(1)}, f32[80,128]{1,0:T(8,128)S(1)}, u32[]{:S(2)}, u32[]{:S(2)}) collective-permute-start(f32[80,128]{1,0:T(8,128)S(1)} %pad_maximum_fusion), channel_id=1, source_target_pairs={{0,16},{16,0},{1,17},{17,1},{2,18},{18,2},{3,19},{19,3},{4,20},{20... | collective-permute-start | bytes 122888 | tf_op jit(solution)/shard_map/ppermute | solution.py:227
  34.3 16.1 %collective-permute-start.1 = (f32[128,128]{1,0:T(8,128)S(1)}, f32[128,128]{1,0:T(8,128)S(1)}, u32[]{:S(2)}, u32[]{:S(2)}) collective-permute-start(f32[128,128]{1,0:T(8,128)S(1)} %slice_bitcast_fusion), channel_id=1, source_target_pairs={{0,16},{16,0},{1,17},{17,1},{2,18},{18,2},{3,19},{19,3},{4,20},{20... | collective-permute-start | bytes 196616 | tf_op jit(solution)/shard_map/ppermute | solution.py:237
  37.2 12.6 %all-to-all-start.2 = ((f32[16,2,128]{2,1,0:T(2,128)}), f32[16,2,128]{2,1,0:T(2,128)S(1)}, u32[]{:S(2)}, u32[]{:S(2)}) async-start(f32[16,2,128]{2,1,0:T(2,128)} %broadcast_in_dim.14), calls=%async_computation.2 | async-start | bytes 32768 | tf_op jit(solution)/shard_map/all_to_all | solution.py:234
  50.4 0.7 %copy-start = (f32[256,128]{1,0:T(8,128)}, f32[256,128]{1,0:T(8,128)S(1)}, u32[]{:S(2)}) copy-start(f32[256,128]{1,0:T(8,128)S(1)} %constant_dynamic-update-slice_fusion) | copy-start | bytes 393220

commit v8 on v5

--- a/solution.py
+++ b/solution.py
@@ -11,6 +11,14 @@
 LOG2E = math.log2(math.e)
 LANES = 128
 SUBLANES = 8
+
+
+FIRST_CHIP = 10
+FIRST_PLACE = 11
+
+
+def led_by(first, count):
+    return [[(first + i) % count for i in range(count)]]
 
 
 def rounded(x):
@@ -168,7 +176,9 @@
 def pick_kernel(utility_ref, shares_ref, chars_ref, coef_ref, taste_ref, half_ref, own_ref, given_ref, scale_ref, side_ref, sems):
     count = half_ref.shape[0]
     markets = own_ref.shape[0] - 2
-    core, chip = lax.axis_index("prod"), lax.axis_index("draw")
+    core = lax.axis_index("prod")
+    chips = lax.axis_size("draw")
+    chip = (lax.axis_index("draw") + (chips - FIRST_CHIP)) % chips
     pairs = [(taste_ref.at[pl.ds(core * count, count)], half_ref), (coef_ref, scale_ref)]
     for ref, side in ((given_ref, 1 - core), (own_ref, core)):
         rows = pl.ds(side * count + chip * markets, markets)
@@ -202,17 +212,18 @@
     half = markets // cores
     own_markets = half // chips
     swap = [(0, 1), (1, 0)]
+    plane, meeting = led_by(FIRST_CHIP, chips), led_by(FIRST_PLACE, planes * cores)
 
     taste, own, given, coef_scale, side = picked(start_utility, log_shares, characteristics, coef_scale, taste_draws, half, own_markets)
     other = lax.ppermute(given, "prod", swap)
-    taste = lax.all_to_all(taste.reshape(chips, own_markets, coefs, LANES), "draw", 0, 0, tiled=True)
+    taste = lax.all_to_all(taste.reshape(chips, own_markets, coefs, LANES), "draw", 0, 0, axis_index_groups=plane, tiled=True)
     gate = taste[0, 0] * 0.5
     blocks = contraction(gate, coef_scale, own, other, taste)
-    blocks = lax.all_to_all(blocks, "draw", 0, 0, tiled=True)
+    blocks = lax.all_to_all(blocks, "draw", 0, 0, axis_index_groups=plane, tiled=True)
 
     squares = jnp.sum(blocks[:, 2 * own_markets : 2 * own_markets + 2], axis=0)
     squares = jnp.broadcast_to(squares, (planes * cores, 2, LANES))
-    squares = lax.all_to_all(squares, ("mkt", "prod"), 0, 0, tiled=True)
+    squares = lax.all_to_all(squares, ("mkt", "prod"), 0, 0, axis_index_groups=meeting, tiled=True)
     given = blocks[:, own_markets : 2 * own_markets].reshape(half, LANES)
     given = lax.ppermute(given, "prod", swap)
     kept = blocks[:, :own_markets].reshape(half, LANES)

time: 59.4 us -> 52 us (0.88)
  waiting for transfers between devices: 23.7 us -> 11.6 us
  starting transfers between devices: 24 us -> 28.8 us
    all_to_all x2, waiting for transfers between devices: 14.3 us -> 5.6 us  [the longest x1 2.82 us: shards(): lax.all_to_all(squares, ('mkt', 'prod'), 0, 0, axis_index_groups=meeting,...]
    all_to_all x1, waiting for transfers between devices: 9.38 us -> 5.96 us  [shards(): lax.all_to_all(taste.reshape(chips, own_markets, coefs, LANES), 'draw', 0...]
    all_to_all x2, starting transfers between devices: 15.2 us -> 17.8 us  [the longest x1 11.1 us: shards(): lax.all_to_all(squares, ('mkt', 'prod'), 0, 0, axis_index_groups=meeting,...]
    all_to_all x1, starting transfers between devices: 7.58 us -> 9.6 us  [shards(): lax.all_to_all(taste.reshape(chips, own_markets, coefs, LANES), 'draw', 0...]
where the time goes in v8:
time: 52 us; the launch traced here: 51.7 us
  starting transfers between devices  28.8 us (55%)
  waiting for transfers between devices  11.6 us (22%)
  Pallas kernels  8.71 us (17%)
  other arithmetic  1.37 us (3%)
  between operations  0.66 us (1%)
  local copies, waits for them, and re-layouts  0.62 us (1%)
    all_to_all x1, starting transfers between devices, shards(): lax.all_to_all(squares, ('mkt', 'prod'), 0, 0, axis_index_groups=meeting,...  11.1 us
    all_to_all x1, starting transfers between devices, shards(): lax.all_to_all(taste.reshape(chips, own_markets, coefs, LANES), 'draw', 0...  9.6 us
    pallas_call x1, Pallas kernels, contraction(): pl.pallas_call(contraction_kernel, out_shape=jax.ShapeDtypeStruct((chips,...  6.78 us
    all_to_all x1, starting transfers between devices, shards(): lax.all_to_all(blocks, 'draw', 0, 0, axis_index_groups=plane, tiled=True)  6.68 us
    all_to_all x1, waiting for transfers between devices, shards(): lax.all_to_all(taste.reshape(chips, own_markets, coefs, LANES), 'draw', 0...  5.96 us
    all_to_all x1, waiting for transfers between devices, shards(): lax.all_to_all(squares, ('mkt', 'prod'), 0, 0, axis_index_groups=meeting,...  2.82 us
    all_to_all x1, waiting for transfers between devices, shards(): lax.all_to_all(blocks, 'draw', 0, 0, axis_index_groups=plane, tiled=True)  2.77 us
    pallas_call x1, Pallas kernels, picked(): pl.pallas_call(pick_kernel, out_shape=[pltpu.VMEM((count, *taste.shape[1:...  1.93 us
  transfers between devices with their start and end apart: 5, of which 3 were waited for; matrix products, arithmetic and copies ran while one was open for 1% of the time, Pallas kernels for 0%

profile of v8, /device:TPU:1, one launch (start us, length us, event | category | flops | bytes accessed | tf_op | source)
XLA Modules:
  0.0 51.7 jit_solution(11678616223689305603)
XLA Ops:
  0.6 1.9 %shard_map.68 = (f32[128,8,128]{2,1,0:T(8,128)}, f32[10,8,128]{2,1,0:T(8,128)S(1)}, f32[10,8,128]{2,1,0:T(8,128)S(1)}, f32[8]{0:T(128)S(1)}, s32[1,128]{1,0:T(1,128)S(1)}) custom-call(f32[256,128]{1,0:T(8,128)} %utility_ref.1, f32[256,128]{1,0:T(8,128)} %shares_ref.1, f32[256,8,128]{2,1,0:T(8,128)} %chars_ref.1, f32[8]{0:T(128)} %coef_ref.1, ...), custom_call_target="tpu_custom_call" | custom-call | tf_op jit(solution)/shard_map/pallas_call | solution.py:200
  2.6 9.6 %all-to-all-start = ((f32[16,8,8,128]{3,2,1,0:T(8,128)}), f32[16,8,8,128]{3,2,1,0:T(8,128)S(1)}, u32[]{:S(2)}, u32[]{:S(2)}) async-start(f32[16,8,8,128]{3,2,1,0:T(8,128)} %bitcast.1), calls=%async_computation | async-start | bytes 1048576 | tf_op jit(solution)/shard_map/all_to_all | solution.py:219
  12.2 1.0 %collective-permute-start = (f32[10,8,128]{2,1,0:T(8,128)S(1)}, f32[10,8,128]{2,1,0:T(8,128)S(1)}, u32[]{:S(2)}, u32[]{:S(2)}) collective-permute-start(f32[10,8,128]{2,1,0:T(8,128)S(1)} %get-tuple-element.11), channel_id=1, source_target_pairs={{0,16},{16,0},{1,17},{17,1},{2,18},{18,2},{3,19},{19,3},{4,20},{20... | collective-permute-start | bytes 122888 | tf_op jit(solution)/shard_map/ppermute | solution.py:218
  13.1 6.0 %all-to-all-done.taste_ref = f32[16,8,8,128]{3,2,1,0:T(8,128)S(1)} async-done(((f32[16,8,8,128]{3,2,1,0:T(8,128)}), f32[16,8,8,128]{3,2,1,0:T(8,128)S(1)}, u32[]{:S(2)}, u32[]{:S(2)}) %all-to-all-start) | async-done | bytes 524320 | tf_op jit(solution)/shard_map/all_to_all | solution.py:219
  19.1 0.0 collective-permute-done.other_ref
  19.1 6.8 %shard_map.69 = f32[16,24,128]{2,1,0:T(8,128)} custom-call(f32[8,128]{1,0:T(8,128)S(1)} %fusion.2.gate_ref, f32[8]{0:T(128)S(1)} %get-tuple-element.9.coef_ref, f32[10,8,128]{2,1,0:T(8,128)S(1)} %get-tuple-element.10.own_ref, f32[10,8,128]{2,1,0:T(8,128)S(1)} %collective-permute-done.other_ref, f32[16,8,8,128]{3,2,1,0:T(8,128)S(1)} %all-to-all-done.taste_ref), custom_call_target="tpu_custom_call" | custom-call | tf_op jit(solution)/shard_map/pallas_call | solution.py:159
  25.9 6.7 %all-to-all-start.1 = ((f32[16,24,128]{2,1,0:T(8,128)}), f32[16,24,128]{2,1,0:T(8,128)S(1)}, u32[]{:S(2)}, u32[]{:S(2)}) async-start(f32[16,24,128]{2,1,0:T(8,128)} %shard_map.69), calls=%async_computation.1 | async-start | bytes 393216 | tf_op jit(solution)/shard_map/all_to_all | solution.py:222
  32.6 2.8 %all-to-all-done.1 = f32[16,24,128]{2,1,0:T(8,128)S(1)} async-done(((f32[16,24,128]{2,1,0:T(8,128)}), f32[16,24,128]{2,1,0:T(8,128)S(1)}, u32[]{:S(2)}, u32[]{:S(2)}) %all-to-all-start.1) | async-done | bytes 196640 | tf_op jit(solution)/shard_map/all_to_all | solution.py:222
  35.4 0.6 %broadcast_in_dim.18 = f32[16,2,128]{2,1,0:T(2,128)} broadcast(f32[2,128]{1,0:T(2,128)S(1)} %slice_reduce_fusion), dimensions={1,2} | broadcast | bytes 17408 | tf_op jit(solution)/shard_map/broadcast_in_dim | solution.py:225
  36.0 11.1 %all-to-all-start.2 = ((f32[16,2,128]{2,1,0:T(2,128)}), f32[16,2,128]{2,1,0:T(2,128)S(1)}, u32[]{:S(2)}, u32[]{:S(2)}) async-start(f32[16,2,128]{2,1,0:T(2,128)} %broadcast_in_dim.18), calls=%async_computation.2 | async-start | bytes 32768 | tf_op jit(solution)/shard_map/all_to_all | solution.py:226
  47.1 0.5 collective-permute-start.1
  47.5 2.8 %all-to-all-done.2 = f32[16,2,128]{2,1,0:T(2,128)S(1)} async-done(((f32[16,2,128]{2,1,0:T(2,128)}), f32[16,2,128]{2,1,0:T(2,128)S(1)}, u32[]{:S(2)}, u32[]{:S(2)}) %all-to-all-start.2) | async-done | bytes 16416 | tf_op jit(solution)/shard_map/all_to_all | solution.py:226
  50.4 0.1 reduce_sum.19
  50.5 0.5 %add_sqrt_fusion = f32[2]{0:T(128)} fusion(f32[2]{0:T(128)S(1)} %reduce_sum.19), kind=kLoop, calls=%fused_computation.9 | loop fusion | flops 4 | bytes 16 | tf_op jit(solution)/shard_map/sqrt | solution.py:233
  51.0 0.0 collective-permute-done.1
  51.0 0.7 %pad_maximum_fusion = f32[256,128]{1,0:T(8,128)} fusion(f32[128,128]{1,0:T(8,128)S(1)} %get-tuple-element.13, f32[128,128]{1,0:T(8,128)S(1)} %get-tuple-element.12), kind=kLoop, calls=%fused_computation | loop fusion | flops 32768 | bytes 262144 | tf_op jit(solution)/shard_map/concatenate | solution.py:231
  (5 shorter events, 0.0 us)
Async XLA Ops:
  2.6 16.5 %all-to-all-start = ((f32[16,8,8,128]{3,2,1,0:T(8,128)}), f32[16,8,8,128]{3,2,1,0:T(8,128)S(1)}, u32[]{:S(2)}, u32[]{:S(2)}) async-start(f32[16,8,8,128]{3,2,1,0:T(8,128)} %bitcast.1), calls=%async_computation | async-start | bytes 1048576 | tf_op jit(solution)/shard_map/all_to_all | solution.py:219
  12.2 6.9 %collective-permute-start = (f32[10,8,128]{2,1,0:T(8,128)S(1)}, f32[10,8,128]{2,1,0:T(8,128)S(1)}, u32[]{:S(2)}, u32[]{:S(2)}) collective-permute-start(f32[10,8,128]{2,1,0:T(8,128)S(1)} %get-tuple-element.11), channel_id=1, source_target_pairs={{0,16},{16,0},{1,17},{17,1},{2,18},{18,2},{3,19},{19,3},{4,20},{20... | collective-permute-start | bytes 122888 | tf_op jit(solution)/shard_map/ppermute | solution.py:218
  25.9 9.5 %all-to-all-start.1 = ((f32[16,24,128]{2,1,0:T(8,128)}), f32[16,24,128]{2,1,0:T(8,128)S(1)}, u32[]{:S(2)}, u32[]{:S(2)}) async-start(f32[16,24,128]{2,1,0:T(8,128)} %shard_map.69), calls=%async_computation.1 | async-start | bytes 393216 | tf_op jit(solution)/shard_map/all_to_all | solution.py:222
  36.0 14.4 %all-to-all-start.2 = ((f32[16,2,128]{2,1,0:T(2,128)}), f32[16,2,128]{2,1,0:T(2,128)S(1)}, u32[]{:S(2)}, u32[]{:S(2)}) async-start(f32[16,2,128]{2,1,0:T(2,128)} %broadcast_in_dim.18), calls=%async_computation.2 | async-start | bytes 32768 | tf_op jit(solution)/shard_map/all_to_all | solution.py:226
  47.1 4.0 %collective-permute-start.1 = (f32[128,128]{1,0:T(8,128)S(1)}, f32[128,128]{1,0:T(8,128)S(1)}, u32[]{:S(2)}, u32[]{:S(2)}) collective-permute-start(f32[128,128]{1,0:T(8,128)S(1)} %slice_bitcast_fusion), channel_id=1, source_target_pairs={{0,16},{16,0},{1,17},{17,1},{2,18},{18,2},{3,19},{19,3},{4,20},{20... | collective-permute-start | bytes 196616 | tf_op jit(solution)/shard_map/ppermute | solution.py:228
